TPU v7x, 32 devices: a whole 2x2x4 slice. The times are simulated.
32 devices in a mesh: rep: 2 (over x), mp: 16 (over z, y, core).
Axes of the slice: x: 2, y: 2, z: 4, core: 2. Of those that a mesh axis runs over, the one named last changes fastest.
Arguments:
- tokens: bfloat16 [1280, 3072], P(('rep', 'mp')), may hold values from -6 to 6
- w_in: bfloat16 [2, 3072, 2, 12288], P('rep', None, None, 'mp'), may hold values from -0.109375 to 0.109375
- w_down: bfloat16 [2, 12288, 3072], P('rep', 'mp'), may hold values from -0.0546875 to 0.0546875
- norm_gain: float32 [3072], replicated, may hold values from 0.1 to 1.9
- final_gain: float32 [3072], replicated, may hold values from 0.1 to 1.9
- value_head: float32 [3072], replicated, may hold values from -0.6 to 0.6
- owner: int32 [16], P('mp'), may hold values from 0 to 1
- lengths: int32 [16], P('rep'), may hold values from 20 to 80, as said below
- offsets: int32 [16], P('rep'), may hold values from 0 to 620, as said below
Outputs:
- mixed: bfloat16 [1280, 3072], P(('rep', 'mp'))
- rewards: float32 [16], P('rep')
Inputs may be any that keep to these rules, and one draw needn't show every extreme that they name: `lengths`: every rollout is at least a quarter of 80 long; in each group one rollout has exactly 80 tokens. `offsets`: rollout j of a group lies wholly within slots j * 80 to (j + 1) * 80 - 1 of its group; the other slots are padding.
All inputs are finite; a program needn't handle non-finite values.
Results may differ from a plain program's by a relative error of at most 0.0046.
Values may be sent and summed in bfloat16 or wider, within the bound.
A program may use at most 128 MiB of HBM per device.

v0:
```python
import functools

import jax
import jax.numpy as jnp
from jax import lax
from jax.experimental import pallas as pl
from jax.experimental.pallas import tpu as pltpu
from jax.sharding import PartitionSpec as P


def spread(value, axis, source):
    kept = jnp.where(lax.axis_index(axis) == source, value, 0).astype(value.dtype)
    return lax.psum(kept, axis)


def membership(slots, lengths, offsets):
    inside = (slots[:, None] >= offsets[None, :]) & (
        slots[:, None] < offsets[None, :] + lengths[None, :]
    )
    return inside.astype(jnp.float32)


def norm_rows(tokens_f, norm_gain):
    return (
        tokens_f
        * lax.rsqrt(jnp.mean(tokens_f * tokens_f, axis=1, keepdims=True) + 1e-06)
        * norm_gain
    ).astype(jnp.bfloat16)


def finish(tokens_f, delta, final_gain, value_head, lengths, offsets):
    tok_rows = tokens_f.shape[0]
    resid = tokens_f + delta
    mixed = resid.astype(jnp.bfloat16)
    final = resid * lax.rsqrt(jnp.mean(resid * resid, axis=1, keepdims=True) + 1e-06) * final_gain
    values = jnp.dot(final, value_head, precision=lax.Precision.HIGHEST)
    own_slots = lax.axis_index("mp") * tok_rows + jnp.arange(tok_rows, dtype=jnp.int32)
    member = membership(own_slots, lengths, offsets)
    partial_sums = jnp.dot(values, member, precision=lax.Precision.HIGHEST)
    totals = lax.psum(partial_sums, "mp")
    rewards = totals / lengths.astype(jnp.float32)
    return (mixed, rewards)


def move_weights(tokens, w_in, w_down, norm_gain, final_gain, value_head, owner, lengths, offsets):
    owner_index = owner[0]
    width = tokens.shape[1]
    hidden_cols = w_in.shape[3]
    tokens_f = tokens.astype(jnp.float32)
    normed = norm_rows(tokens_f, norm_gain)
    inner_local, outer_local = (
        spread(w_in, "rep", owner_index),
        spread(w_down, "rep", owner_index),
    )
    inner_matrix = inner_local.reshape(width, 2 * hidden_cols)
    piece = lax.all_gather(normed, "mp", axis=0, tiled=True)
    slots = jnp.arange(piece.shape[0], dtype=jnp.int32)
    row_count = piece.shape[0]
    products = jnp.dot(piece, inner_matrix, preferred_element_type=jnp.float32).reshape(
        row_count, 2, hidden_cols
    )
    gate_part = products[:, 0, :]
    up_part = products[:, 1, :]
    hidden = (
        jax.nn.gelu(gate_part, approximate=True)
        * up_part
        * jnp.sum(membership(slots, lengths, offsets), axis=1)[:, None]
    ).astype(jnp.bfloat16)
    outer_matrix = outer_local.reshape(hidden_cols, width)
    delta = lax.psum_scatter(
        jnp.dot(hidden, outer_matrix, preferred_element_type=jnp.float32),
        "mp",
        scatter_dimension=0,
        tiled=True,
    )
    return finish(tokens_f, delta, final_gain, value_head, lengths, offsets)


MESH = pl.DeviceIdType.MESH


def place(half):
    rep, slot = lax.axis_index("rep"), lax.axis_index("mp")
    side, row, level = slot % 2, (slot // 2) % 2, slot // 4
    other_rep, other_row = 1 - rep, 1 - row
    first = (rep * side + other_rep * (1 - side), row * (1 - side) + other_row * side)
    second = (rep * (1 - side) + other_rep * side, row * side + other_row * (1 - side))
    return rep, slot, side, level, (rep, row), first, second, (other_rep, other_row)


def remote(src, dst, send_sem, recv_sem, column, level, side):
    return pltpu.make_async_remote_copy(
        src_ref=src, dst_ref=dst, send_sem=send_sem, recv_sem=recv_sem,
        device_id=(column[0], level * 4 + column[1] * 2 + side), device_id_type=MESH,
    )


def gather_kernel(half, own_ref, out_ref, level_send, first_send, second_send, cross_send, pass_send, recv_sem, local_sem):
    rep, slot, side, level, here, first, second, cross = place(half)
    levels = half // 2

    barrier = pltpu.get_barrier_semaphore()

    def greet(column, at, plane):
        pl.semaphore_signal(
            barrier, inc=1, device_id=(column[0], at * 4 + column[1] * 2 + plane), device_id_type=MESH
        )

    greet(first, level, side)
    greet(second, level, side)
    greet(here, level, 1 - side)

    @pl.loop(1, levels)
    def _(d):
        greet(here, (level + d) % levels, side)

    pl.semaphore_wait(barrier, levels + 2)

    def index_of(column, at):
        return (column[0] * half + at * 2 + column[1]) * 2 + side

    mine = index_of(here, level)

    def from_level(d):
        return (level + levels - d) % levels

    def climb(d):
        return remote(own_ref, out_ref.at[mine], level_send.at[d], recv_sem.at[mine], here, (level + d) % levels, side)

    def move(src, index, sem, column):
        return remote(src, out_ref.at[index], sem, recv_sem.at[index], column, level, side)

    def hand(src, index):
        return remote(src, out_ref.at[index], pass_send.at[index], recv_sem.at[index], here, level, 1 - side)

    def arrive(index):
        pltpu.make_async_copy(own_ref, out_ref.at[index], recv_sem.at[index]).wait()

    move(own_ref, mine, first_send.at[0], first).start()

    @pl.loop(1, levels)
    def _(d):
        climb(d).start()

    move(own_ref, mine, second_send.at[0], second).start()
    hand(own_ref, mine).start()
    keep = pltpu.make_async_copy(own_ref, out_ref.at[mine], local_sem)
    keep.start()

    def relay(d):
        index = index_of(first, from_level(d))
        arrive(index)
        move(out_ref.at[index], index, cross_send.at[d], second).start()
        hand(out_ref.at[index], index).start()

    def settle(d):
        for column in (second, cross):
            index = index_of(column, from_level(d))
            arrive(index)
            hand(out_ref.at[index], index).start()

    relay(0)

    @pl.loop(1, levels)
    def _(d):
        index = index_of(here, from_level(d))
        arrive(index)
        move(out_ref.at[index], index, first_send.at[d], first).start()
        move(out_ref.at[index], index, second_send.at[d], second).start()
        hand(out_ref.at[index], index).start()
        relay(d)
        settle(d - 1)

    settle(levels - 1)

    @pl.loop(0, 2 * half)
    def _(i):
        arrive(2 * i + 1 - side)

    keep.wait()

    @pl.loop(1, levels)
    def _(d):
        climb(d).wait_send()

    @pl.loop(0, levels)
    def _(d):
        for sem in (first_send, second_send, cross_send):
            move(own_ref, mine, sem.at[d], first).wait_send()

    @pl.loop(0, 2 * half)
    def _(i):
        hand(own_ref, 2 * i + side).wait_send()


def gather_rows(own, half):
    dma = pltpu.SemaphoreType.DMA
    levels = half // 2
    return pl.pallas_call(
        functools.partial(gather_kernel, half),
        out_shape=jax.ShapeDtypeStruct((4 * half,) + own.shape, own.dtype),
        in_specs=[pl.BlockSpec(memory_space=pltpu.VMEM)],
        out_specs=pl.BlockSpec(memory_space=pl.ANY),
        scratch_shapes=[
            dma((levels,)), dma((levels,)), dma((levels,)), dma((levels,)),
            dma((4 * half,)), dma((4 * half,)), dma,
        ],
        compiler_params=pltpu.CompilerParams(collective_id=0, has_side_effects=True),
    )(own)


def reduce_kernel(half, part_ref, tok_ref, live_ref, member_ref, final_ref, head_ref, mixed_ref, totals_ref,
                  swap_buf, mine_buf, sum_buf, cross_buf, first_buf, second_buf, level_buf, acc, mean_buf, own_mean,
                  swap_send, swap_recv, local_sem, send_sem, cross_recv, first_recv, second_recv, level_recv,
                  mean_send, mean_recv):
    rep, slot, side, level, here, first, second, cross = place(half)
    levels, parts = half // 2, 2 * half
    barrier = pltpu.get_barrier_semaphore()
    pl.semaphore_signal(barrier, inc=1, device_id=(1 - rep, slot), device_id_type=MESH)

    @pl.loop(1, parts)
    def _(d):
        pl.semaphore_signal(barrier, inc=1, device_id=(rep, (slot + d) % parts), device_id_type=MESH)

    pl.semaphore_wait(barrier, parts)

    def target(column, d):
        return column[0] * half + ((level + d) % levels) * 2 + column[1]

    def swap(to):
        return remote(
            part_ref.at[2 * to + 1 - side], swap_buf.at[to], swap_send.at[to], swap_recv.at[to], here, level, 1 - side
        )

    def fetch(to):
        return pltpu.make_async_copy(part_ref.at[2 * to + side], mine_buf.at[to], local_sem.at[to])

    def send(to, buf, sem, slot_at, column, at):
        return remote(sum_buf.at[to], buf.at[slot_at], send_sem.at[to], sem.at[slot_at], column, at, side)

    def arrive(buf, sem, at):
        pltpu.make_async_copy(sum_buf.at[0], buf.at[at], sem.at[at]).wait()

    def both(to):
        fetch(to).wait()
        swap(to).wait_recv()
        return mine_buf[to].astype(jnp.float32) + swap_buf[to].astype(jnp.float32)

    def start(to):
        swap(to).start()
        fetch(to).start()

    @pl.loop(1, levels + 1)
    def _(d):
        start(target(cross, d))
        start(target(second, d))

    @pl.loop(1, levels + 1)
    def _(d):
        start(target(first, d))
        start(target(here, d))

    @pl.loop(1, levels + 1)
    def _(d):
        at = (level + d) % levels
        to = target(cross, d)
        sum_buf[to] = both(to).astype(jnp.bfloat16)
        send(to, cross_buf, cross_recv, at, second, level).start()
        to = target(second, d)
        sum_buf[to] = both(to).astype(jnp.bfloat16)
        send(to, second_buf, second_recv, at, second, level).start()

    @pl.loop(1, levels + 1)
    def _(d):
        at = (level + d) % levels
        to = target(first, d)
        mine = both(to)
        arrive(cross_buf, cross_recv, at)
        sum_buf[to] = (mine + cross_buf[at].astype(jnp.float32)).astype(jnp.bfloat16)
        send(to, first_buf, first_recv, at, first, level).start()

    def collect(d):
        at = (level + d) % levels
        mine = both(target(here, d))
        arrive(second_buf, second_recv, at)
        arrive(first_buf, first_recv, at)
        return mine + (second_buf[at].astype(jnp.float32) + first_buf[at].astype(jnp.float32))

    @pl.loop(1, levels)
    def _(d):
        to = target(here, d)
        sum_buf[to] = collect(d).astype(jnp.bfloat16)
        send(to, level_buf, level_recv, level, here, (level + d) % levels).start()

    acc[...] = collect(0)

    @pl.loop(1, levels)
    def _(d):
        at = (level + levels - d) % levels
        arrive(level_buf, level_recv, at)
        acc[...] += level_buf[at].astype(jnp.float32)

    resid = tok_ref[...].astype(jnp.float32) + acc[...] * live_ref[...]
    mixed_ref[...] = resid.astype(jnp.bfloat16)
    scale = lax.rsqrt(jnp.mean(resid * resid, axis=1, keepdims=True) + 1e-06)
    values = jnp.sum(resid * scale * final_ref[...] * head_ref[...], axis=1, keepdims=True)
    own_mean[...] = jnp.broadcast_to(jnp.sum(values * member_ref[...], axis=0, keepdims=True), own_mean.shape)

    def tell(d):
        to = (slot + d) % parts
        return pltpu.make_async_remote_copy(
            src_ref=own_mean, dst_ref=mean_buf.at[slot], send_sem=mean_send.at[to],
            recv_sem=mean_recv.at[slot], device_id=(rep, to), device_id_type=MESH,
        )

    @pl.loop(1, parts)
    def _(d):
        tell(d).start()

    totals_ref[...] = own_mean[...]

    @pl.loop(1, parts)
    def _(d):
        index = (slot + parts - d) % parts
        pltpu.make_async_copy(own_mean, mean_buf.at[index], mean_recv.at[index]).wait()
        totals_ref[...] += mean_buf[index]

    @pl.loop(0, levels)
    def _(d):
        for column in (cross, second, first, here):
            swap(target(column, d)).wait_send()
        for column in (cross, second, first):
            send(target(column, d), cross_buf, cross_recv, level, second, level).wait_send()

    @pl.loop(1, levels)
    def _(d):
        send(target(here, d), level_buf, level_recv, level, second, level).wait_send()

    @pl.loop(1, parts)
    def _(d):
        tell(d).wait_send()


def reduce_rows(part, tokens, live, member, final_gain, value_head, half):
    shape = tokens.shape
    levels, chips, parts = half // 2, 2 * half, 2 * half
    vmem = pl.BlockSpec(memory_space=pltpu.VMEM)
    dma = pltpu.SemaphoreType.DMA
    block = pltpu.VMEM((chips,) + shape, jnp.bfloat16)
    few = pltpu.VMEM((levels,) + shape, jnp.bfloat16)
    return pl.pallas_call(
        functools.partial(reduce_kernel, half),
        out_shape=(
            jax.ShapeDtypeStruct(shape, jnp.bfloat16),
            jax.ShapeDtypeStruct((8, 128), jnp.float32),
        ),
        in_specs=[pl.BlockSpec(memory_space=pl.ANY)] + [vmem] * 5,
        out_specs=(vmem, vmem),
        scratch_shapes=[
            block, block, block, few, few, few, few,
            pltpu.VMEM(shape, jnp.float32),
            pltpu.VMEM((parts, 8, 128), jnp.float32),
            pltpu.VMEM((8, 128), jnp.float32),
            dma((chips,)), dma((chips,)), dma((chips,)), dma((chips,)),
            dma((levels,)), dma((levels,)), dma((levels,)), dma((levels,)),
            dma((parts,)), dma((parts,)),
        ],
        compiler_params=pltpu.CompilerParams(
            collective_id=1, has_side_effects=True, vmem_limit_bytes=48 << 20
        ),
    )(part, tokens, live, member, final_gain[None, :], value_head[None, :])


def move_rows(reps, parts, tokens, w_in, w_down, norm_gain, final_gain, value_head, owner, lengths, offsets):
    tok_rows, width = tokens.shape
    half = parts // 2
    normed = norm_rows(tokens.astype(jnp.float32), norm_gain)
    rows = gather_rows(normed, half).reshape(reps * parts * tok_rows, width)
    cols = w_in.shape[3]
    products = jnp.dot(rows, w_in.reshape(width, 2 * cols), preferred_element_type=jnp.float32)
    gate, up = products[:, :cols], products[:, cols:]
    mine = owner[0] == lax.axis_index("rep")
    hidden = jnp.where(mine, jax.nn.gelu(gate, approximate=True) * up, 0.0).astype(jnp.bfloat16)
    hidden = lax.optimization_barrier(hidden)
    part = jnp.dot(hidden, w_down[0], preferred_element_type=jnp.float32).astype(jnp.bfloat16)
    own_slots = lax.axis_index("mp") * tok_rows + jnp.arange(tok_rows, dtype=jnp.int32)
    member = membership(own_slots, lengths, offsets)
    live = jnp.sum(member, axis=1)[:, None]
    count = lengths.shape[0]
    member = jnp.pad(member, ((0, 0), (0, 128 - count)))
    mixed, totals = reduce_rows(
        part.reshape(reps * parts, tok_rows, width), tokens, live, member, final_gain, value_head, half
    )
    return mixed, totals[0, :count] / lengths.astype(jnp.float32)


def lengths_fit(args):
    return args[7].shape[0] <= 128


def per_device(reps, parts, *args):
    tokens, w_in, w_down = args[:3]
    row_bytes = 2 * reps * parts * tokens.size * 2
    weight_bytes = 2 * (w_in.size + w_down.size)
    if reps == 2 and parts % 4 == 0 and lengths_fit(args) and row_bytes < 2 * weight_bytes:
        return move_rows(reps, parts, *args)
    return move_weights(*args)


def solution(mesh):
    in_specs = (
        P(("rep", "mp"), None),
        P("rep", None, None, "mp"),
        P("rep", "mp", None),
        P(),
        P(),
        P(),
        P("mp"),
        P("rep"),
        P("rep"),
    )
    out_specs = (P(("rep", "mp"), None), P("rep"))
    return jax.shard_map(
        functools.partial(per_device, mesh.shape["rep"], mesh.shape["mp"]),
        mesh=mesh, in_specs=in_specs, out_specs=out_specs, check_vma=False,
    )
```

profile of v0, /device:TPU:0, one launch (start us, length us, event | category | flops | bytes accessed | tf_op | source)
XLA Modules:
  0.0 163.1 jit_solution(9352128747379156161)
XLA Ops:
  0.6 1.1 fusion.11
  1.7 1.8 %fusion.13.own_ref = bf16[40,3072]{1,0:T(8,128)(2,1)} fusion(bf16[40,3072]{1,0:T(8,128)(2,1)} %tok_ref.1, f32[3072]{0:T(1024)} %param.12, f32[40]{0:T(128)S(1)} %add_rsqrt_fusion), kind=kLoop, calls=%fused_computation.17 | loop fusion | flops 491520 | bytes 503968 | tf_op jit(solution)/shard_map/convert_element_type | solution.py:28
  3.5 46.0 %shard_map.104 = bf16[32,40,3072]{2,1,0:T(8,128)(2,1)} custom-call(bf16[40,3072]{1,0:T(8,128)(2,1)} %fusion.13.own_ref), custom_call_target="tpu_custom_call" | custom-call | tf_op jit(solution)/shard_map/pallas_call | solution.py:199
  49.5 9.0 %copy.15 = bf16[384,8,2,768]{3,1,2,0:T(8,128)(2,1)} copy(bf16[384,8,2,768]{3,2,1,0:T(2,128)(2,1)} %bitcast.20) | data formatting | bytes 18874368
  58.5 18.5 %fusion.15 = f32[1280,1536]{1,0:T(8,128)} fusion(bf16[1280,3072]{1,0:T(8,128)(2,1)} %bitcast.23, bf16[3072,1536]{1,0:T(8,128)(2,1)} %bitcast.21), kind=kOutput, calls=%fused_computation.23 | convolution fusion | flops 12079595520 | bytes 25165824 | tf_op jit(solution)/shard_map/dot_general | solution.py:380
  77.7 4.1 %fusion.10 = bf16[1280,768]{1,0:T(8,128)(2,1)S(1)} fusion(f32[1280,1536]{1,0:T(8,128)} %fusion.15, pred[]{:T(512)S(6)} %eq.3), kind=kLoop, calls=%fused_computation.12 | loop fusion | flops 10813440 | bytes 9830401 | tf_op jit(solution)/shard_map/convert_element_type | solution.py:383
  81.8 0.0 copy-start.3
  81.8 0.0 copy-start.4
  81.8 0.0 copy-start
  81.8 0.0 copy-start.1
  81.8 0.0 copy-start.2
  81.8 10.8 %convolution_convert_fusion = bf16[1280,3072]{1,0:T(8,128)(2,1)} fusion(bf16[1280,768]{1,0:T(8,128)(2,1)S(1)} %fusion.10, bf16[1,768,3072]{2,1,0:T(8,128)(2,1)} %param.11), kind=kOutput, calls=%fused_computation | convolution fusion | flops 6043729920 | bytes 14548992 | tf_op jit(solution)/shard_map/dot_general | solution.py:385
  92.6 0.0 copy-done.3
  92.6 0.0 copy-done.4
  92.6 0.2 fusion.14
  92.8 0.1 copy.14.live_ref
  92.9 0.1 and_convert_fusion
  93.0 0.0 copy-done
  93.0 0.0 copy-done.1
  93.0 0.0 copy-done.2
  93.0 68.8 %shard_map.105 = (bf16[40,3072]{1,0:T(8,128)(2,1)S(1)}, f32[8,128]{1,0:T(8,128)S(1)}) custom-call(bf16[32,40,3072]{2,1,0:T(8,128)(2,1)} %bitcast.22, bf16[40,3072]{1,0:T(8,128)(2,1)S(1)} %copy-done, f32[40,1]{1,0:T(8,128)S(1)} %copy.14.live_ref, f32[40,128]{1,0:T(8,128)S(1)} %pad.4.member_ref, f32[1,3072]{1,0:T(1,128)S(1)} %bitcast.18, f32[1,3072]{1,0:T(1,128)S(1)} %bitcast.19), custom_call_target="tpu_custom_call" | custom-call | tf_op jit(solution)/shard_map/pallas_call | solution.py:351
  161.8 0.5 bitcast_divide_fusion
  162.4 0.7 copy.18
  (4 shorter events, 0.0 us)
Async XLA Ops:
  81.8 10.9 %copy-start.3 = (s32[8]{0:T(128)S(1)}, s32[8]{0:T(128)}, u32[]{:S(2)}) copy-start(s32[8]{0:T(128)} %param.17) | copy-start | bytes 100
  81.8 10.8 %copy-start.4 = (s32[8]{0:T(128)S(1)}, s32[8]{0:T(128)}, u32[]{:S(2)}) copy-start(s32[8]{0:T(128)} %param.16) | copy-start | bytes 100
  81.8 11.2 %copy-start = (bf16[40,3072]{1,0:T(8,128)(2,1)S(1)}, bf16[40,3072]{1,0:T(8,128)(2,1)}, u32[]{:S(2)}) copy-start(bf16[40,3072]{1,0:T(8,128)(2,1)} %tok_ref.1) | copy-start | bytes 737284
  81.8 11.2 %copy-start.1 = (f32[3072]{0:T(1024)S(1)}, f32[3072]{0:T(1024)}, u32[]{:S(2)}) copy-start(f32[3072]{0:T(1024)} %param.13) | copy-start | bytes 36868
  81.8 11.2 %copy-start.2 = (f32[3072]{0:T(1024)S(1)}, f32[3072]{0:T(1024)}, u32[]{:S(2)}) copy-start(f32[3072]{0:T(1024)} %param.14) | copy-start | bytes 36868
where the time goes:
time: 163 us
  Pallas kernels  115 us (71%)
  matrix products  29.3 us (18%)
  local copies, waits for them, and re-layouts  9.79 us (6%)
  other arithmetic  7.73 us (5%)
    pallas_call x1, Pallas kernels, reduce_rows(): pl.pallas_call(functools.partial(reduce_kernel, half), out_shape=(jax.Sha...  68.8 us
    pallas_call x1, Pallas kernels, gather_rows(): pl.pallas_call(functools.partial(gather_kernel, half), out_shape=jax.Shap...  46 us
    dot_general x1, matrix products, move_rows(): jnp.dot(rows, w_in.reshape(width, 2 * cols), preferred_element_type=jnp.f...  18.5 us
    dot_general x1, matrix products, move_rows(): jnp.dot(hidden, w_down[0], preferred_element_type=jnp.float32)  10.8 us
    unnamed x12, local copies, waits for them, and re-layouts  9.69 us
    convert_element_type x1, other arithmetic, move_rows(): jnp.where(mine, jax.nn.gelu(gate, approximate=True) * up, 0.0)  4.07 us

commit v1 on v0

v1 whole, which is shorter than its diff:
```python
import functools

import jax
import jax.numpy as jnp
from jax import lax
from jax.experimental import pallas as pl
from jax.experimental.pallas import tpu as pltpu
from jax.sharding import PartitionSpec as P


def spread(value, axis, source):
    kept = jnp.where(lax.axis_index(axis) == source, value, 0).astype(value.dtype)
    return lax.psum(kept, axis)


def membership(slots, lengths, offsets):
    inside = (slots[:, None] >= offsets[None, :]) & (
        slots[:, None] < offsets[None, :] + lengths[None, :]
    )
    return inside.astype(jnp.float32)


def norm_rows(tokens_f, norm_gain):
    return (
        tokens_f
        * lax.rsqrt(jnp.mean(tokens_f * tokens_f, axis=1, keepdims=True) + 1e-06)
        * norm_gain
    ).astype(jnp.bfloat16)


def finish(tokens_f, delta, final_gain, value_head, lengths, offsets):
    tok_rows = tokens_f.shape[0]
    resid = tokens_f + delta
    mixed = resid.astype(jnp.bfloat16)
    final = resid * lax.rsqrt(jnp.mean(resid * resid, axis=1, keepdims=True) + 1e-06) * final_gain
    values = jnp.dot(final, value_head, precision=lax.Precision.HIGHEST)
    own_slots = lax.axis_index("mp") * tok_rows + jnp.arange(tok_rows, dtype=jnp.int32)
    member = membership(own_slots, lengths, offsets)
    partial_sums = jnp.dot(values, member, precision=lax.Precision.HIGHEST)
    totals = lax.psum(partial_sums, "mp")
    rewards = totals / lengths.astype(jnp.float32)
    return (mixed, rewards)


def move_weights(tokens, w_in, w_down, norm_gain, final_gain, value_head, owner, lengths, offsets):
    owner_index = owner[0]
    width = tokens.shape[1]
    hidden_cols = w_in.shape[3]
    tokens_f = tokens.astype(jnp.float32)
    normed = norm_rows(tokens_f, norm_gain)
    inner_local, outer_local = (
        spread(w_in, "rep", owner_index),
        spread(w_down, "rep", owner_index),
    )
    inner_matrix = inner_local.reshape(width, 2 * hidden_cols)
    piece = lax.all_gather(normed, "mp", axis=0, tiled=True)
    slots = jnp.arange(piece.shape[0], dtype=jnp.int32)
    row_count = piece.shape[0]
    products = jnp.dot(piece, inner_matrix, preferred_element_type=jnp.float32).reshape(
        row_count, 2, hidden_cols
    )
    gate_part = products[:, 0, :]
    up_part = products[:, 1, :]
    hidden = (
        jax.nn.gelu(gate_part, approximate=True)
        * up_part
        * jnp.sum(membership(slots, lengths, offsets), axis=1)[:, None]
    ).astype(jnp.bfloat16)
    outer_matrix = outer_local.reshape(hidden_cols, width)
    delta = lax.psum_scatter(
        jnp.dot(hidden, outer_matrix, preferred_element_type=jnp.float32),
        "mp",
        scatter_dimension=0,
        tiled=True,
    )
    return finish(tokens_f, delta, final_gain, value_head, lengths, offsets)


MESH = pl.DeviceIdType.MESH


def mega_kernel(levels, tok_ref, gain_ref, mine_ref, live_ref, member_ref, final_ref, head_ref, win_ref, wdown_ref,
                mixed_ref, totals_ref,
                x_buf, part, swap_buf, sum_buf, cross_buf, first_buf, second_buf, level_buf, win, wdown, hid,
                nrm, stage, acc, delta, mean_buf, own_mean,
                w_sem, half_send, half_recv, level_send, first_send, second_send, cross_send, pass_send, recv_sem,
                swap_send, swap_recv, sum_send, cross_recv, first_recv, second_recv, level_recv, back_send, back_recv,
                mean_send, mean_recv):
    rep, slot = lax.axis_index("rep"), lax.axis_index("mp")
    side, row, level = slot % 2, (slot // 2) % 2, slot // 4
    parts = levels * 4
    other_rep, other_row, twin = 1 - rep, 1 - row, 1 - side
    here, cross = (rep, row), (other_rep, other_row)
    first = (rep * side + other_rep * twin, row * twin + other_row * side)
    second = (rep * twin + other_rep * side, row * side + other_row * twin)
    tok_rows, width = tok_ref.shape
    rows, half = 2 * tok_rows, width // 2
    cols = wdown.shape[0]

    def index_of(column, at):
        return at * 4 + column[0] * 2 + column[1]

    def remote(src, dst, send_sem, recv_sem, column, at, plane):
        return pltpu.make_async_remote_copy(
            src_ref=src, dst_ref=dst, send_sem=send_sem, recv_sem=recv_sem,
            device_id=(column[0], at * 4 + column[1] * 2 + plane), device_id_type=MESH,
        )

    barrier = pltpu.get_barrier_semaphore()
    pl.semaphore_signal(barrier, inc=1, device_id=(other_rep, slot), device_id_type=MESH)

    @pl.loop(1, parts)
    def _(d):
        pl.semaphore_signal(barrier, inc=1, device_id=(rep, (slot + d) % parts), device_id_type=MESH)

    load_in = pltpu.make_async_copy(win_ref, win, w_sem.at[0])
    load_down = pltpu.make_async_copy(wdown_ref, wdown, w_sem.at[1])
    load_in.start()
    load_down.start()

    mine = index_of(here, level)
    my_rows = pl.ds(pl.multiple_of(side * tok_rows, 8), tok_rows)
    twin_rows = pl.ds(pl.multiple_of(twin * tok_rows, 8), tok_rows)
    my_cols = pl.ds(pl.multiple_of(side * half, 128), half)
    twin_cols = pl.ds(pl.multiple_of(twin * half, 128), half)

    tok = tok_ref[...].astype(jnp.float32)
    nrm[...] = tok * lax.rsqrt(jnp.mean(tok * tok, axis=1, keepdims=True) + 1e-06) * gain_ref[...]

    pl.semaphore_wait(barrier, parts)

    trade = remote(nrm.at[:, twin_cols], stage.at[my_rows], half_send, half_recv, here, level, twin)
    trade.start()
    stage[my_rows, :] = nrm[:, my_cols]
    trade.wait_recv()
    x_buf[side, mine] = stage[...].astype(jnp.bfloat16)

    def from_level(d):
        return (level + levels - d) % levels

    def piece(index):
        return x_buf.at[side, index]

    def move(index, sem, column, at):
        return remote(piece(index), piece(index), sem, recv_sem.at[side, index], column, at, side)

    def climb(d):
        return move(mine, level_send.at[d], here, (level + d) % levels)

    def hand(index):
        return remote(piece(index), piece(index), pass_send.at[index], recv_sem.at[side, index], here, level, twin)

    def arrive(plane, index):
        pltpu.make_async_copy(x_buf.at[plane, index], x_buf.at[plane, index], recv_sem.at[plane, index]).wait()

    move(mine, first_send.at[0], first, level).start()
    move(mine, second_send.at[0], second, level).start()

    @pl.loop(1, levels)
    def _(d):
        climb(d).start()

    hand(mine).start()

    def relay(d):
        index = index_of(first, from_level(d))
        arrive(side, index)
        move(index, cross_send.at[d], second, level).start()
        hand(index).start()

    def descend(d):
        index = index_of(here, from_level(d))
        arrive(side, index)
        move(index, first_send.at[d], first, level).start()
        move(index, second_send.at[d], second, level).start()
        hand(index).start()

    def settle(d):
        for column in (second, cross):
            index = index_of(column, from_level(d))
            arrive(side, index)
            hand(index).start()

    def collect_hands(d):
        for column in (here, first, second, cross):
            arrive(twin, index_of(column, from_level(d)))

    def at_level(buf, plane, at):
        return buf[plane, pl.ds(at * 4, 4)]

    up_block = 256

    def up(d):
        at = from_level(d)

        @pl.loop(0, cols // up_block)
        def _(n):
            lo = pl.multiple_of(n * up_block, up_block)

            def dot(offset):
                span = pl.ds(lo + offset, up_block)
                left = at_level(x_buf, 0, at).reshape(4 * rows, half)
                right = at_level(x_buf, 1, at).reshape(4 * rows, half)
                return (jnp.dot(left, win[:half, span], preferred_element_type=jnp.float32)
                        + jnp.dot(right, win[half:, span], preferred_element_type=jnp.float32))

            gate, lift = dot(0), dot(cols)
            hid[:, pl.ds(lo, up_block)] = (
                jax.nn.gelu(gate, approximate=True) * lift * mine_ref[...]
            ).astype(jnp.bfloat16)

    down_block = 512

    def down(d, plane):
        at = from_level(d)

        @pl.loop(0, half // down_block)
        def _(n):
            lo = pl.multiple_of(n * down_block, down_block)
            out = jnp.dot(hid[...], wdown[:, pl.ds(pl.multiple_of(plane * half + lo, down_block), down_block)],
                          preferred_element_type=jnp.float32)
            part[plane, pl.ds(at * 4, 4), :, pl.ds(lo, down_block)] = out.astype(jnp.bfloat16).reshape(
                4, rows, down_block)

    def swap(index):
        return remote(part.at[twin, index], swap_buf.at[index], swap_send.at[index], swap_recv.at[index], here, level, twin)

    def send(index, buf, sem, at, column, to):
        return remote(sum_buf.at[index], buf.at[at], sum_send.at[index], sem.at[at], column, to, side)

    def landed(buf, sem, at):
        pltpu.make_async_copy(buf.at[at], buf.at[at], sem.at[at]).wait()

    def both(index):
        swap(index).wait_recv()
        return part[side, index].astype(jnp.float32) + swap_buf[index].astype(jnp.float32)

    def start_swaps(d):
        for column in (cross, second, first, here):
            swap(index_of(column, from_level(d))).start()

    def reduce_outer(d):
        at = from_level(d)
        for column, buf, sem in ((cross, cross_buf, cross_recv), (second, second_buf, second_recv)):
            index = index_of(column, at)
            sum_buf[index] = both(index).astype(jnp.bfloat16)
            send(index, buf, sem, at, second, level).start()

    def reduce_first(d):
        at = from_level(d)
        index = index_of(first, at)
        total = both(index)
        landed(cross_buf, cross_recv, at)
        sum_buf[index] = (total + cross_buf[at].astype(jnp.float32)).astype(jnp.bfloat16)
        send(index, first_buf, first_recv, at, first, level).start()

    def reduce_here(d):
        at = from_level(d)
        index = index_of(here, at)
        total = both(index)
        landed(second_buf, second_recv, at)
        landed(first_buf, first_recv, at)
        total = total + (second_buf[at].astype(jnp.float32) + first_buf[at].astype(jnp.float32))
        if d == 0:
            acc[...] = total
        else:
            sum_buf[index] = total.astype(jnp.bfloat16)
            send(index, level_buf, level_recv, level, here, at).start()

    relay(0)
    descend(1)
    settle(0)
    collect_hands(0)
    load_in.wait()
    load_down.wait()

    for d in range(levels):
        up(d)
        if d + 1 < levels:
            relay(d + 1)
        if d + 2 < levels:
            descend(d + 2)
        if d >= 1:
            reduce_first(d - 1)
        if d >= 2:
            reduce_here(d - 2)
        down(d, twin)
        start_swaps(d)
        down(d, side)
        if d + 1 < levels:
            settle(d + 1)
        reduce_outer(d)
        if d + 1 < levels:
            collect_hands(d + 1)

    if levels >= 2:
        reduce_here(levels - 2)
    reduce_first(levels - 1)
    reduce_here(levels - 1)

    @pl.loop(1, levels)
    def _(d):
        at = (level + d) % levels
        landed(level_buf, level_recv, at)
        acc[...] += level_buf[at].astype(jnp.float32)

    back = remote(acc.at[twin_rows], delta.at[:, my_cols], back_send, back_recv, here, level, twin)
    back.start()
    delta[:, my_cols] = acc[my_rows, :]
    back.wait_recv()
    resid = tok_ref[...].astype(jnp.float32) + delta[...] * live_ref[...]
    mixed_ref[...] = resid.astype(jnp.bfloat16)
    scale = lax.rsqrt(jnp.mean(resid * resid, axis=1, keepdims=True) + 1e-06)
    values = jnp.sum(resid * scale * final_ref[...] * head_ref[...], axis=1, keepdims=True)
    own_mean[...] = jnp.broadcast_to(jnp.sum(values * member_ref[...], axis=0, keepdims=True), own_mean.shape)

    def tell(d):
        to = (slot + d) % parts
        return pltpu.make_async_remote_copy(
            src_ref=own_mean, dst_ref=mean_buf.at[slot], send_sem=mean_send.at[to],
            recv_sem=mean_recv.at[slot], device_id=(rep, to), device_id_type=MESH,
        )

    @pl.loop(1, parts)
    def _(d):
        tell(d).start()

    totals_ref[...] = own_mean[...]

    trade.wait_send()
    back.wait_send()

    @pl.loop(0, levels)
    def _(d):
        for sem in (first_send, second_send, cross_send):
            move(mine, sem.at[d], first, level).wait_send()

    @pl.loop(1, levels)
    def _(d):
        climb(d).wait_send()

    @pl.loop(0, parts)
    def _(i):
        hand(i).wait_send()
        swap(i).wait_send()

    @pl.loop(0, levels)
    def _(d):
        for column in (cross, second, first):
            send(index_of(column, d), cross_buf, cross_recv, level, second, level).wait_send()

    @pl.loop(1, levels)
    def _(d):
        send(index_of(here, from_level(d)), level_buf, level_recv, level, second, level).wait_send()

    @pl.loop(1, parts)
    def _(d):
        index = (slot + parts - d) % parts
        pltpu.make_async_copy(own_mean, mean_buf.at[index], mean_recv.at[index]).wait()
        totals_ref[...] += mean_buf[index]

    @pl.loop(1, parts)
    def _(d):
        tell(d).wait_send()


def mega_rows(reps, parts, tokens, w_in, w_down, norm_gain, final_gain, value_head, owner, lengths, offsets):
    tok_rows, width = tokens.shape
    cols = w_in.shape[3]
    levels, half, rows = parts // 4, width // 2, 2 * tok_rows
    own_slots = lax.axis_index("mp") * tok_rows + jnp.arange(tok_rows, dtype=jnp.int32)
    member = membership(own_slots, lengths, offsets)
    live = jnp.sum(member, axis=1)[:, None]
    count = lengths.shape[0]
    member = jnp.pad(member, ((0, 0), (0, 128 - count)))
    mine = jnp.broadcast_to((owner == lax.axis_index("rep")).astype(jnp.float32)[:, None], (1, 256))
    vmem = pl.BlockSpec(memory_space=pltpu.VMEM)
    hbm = pl.BlockSpec(memory_space=pl.ANY)
    dma = pltpu.SemaphoreType.DMA
    chips = parts
    f32, bf16 = jnp.float32, jnp.bfloat16

    def units(count):
        return pltpu.VMEM((count, rows, half), bf16)

    mixed, totals = pl.pallas_call(
        functools.partial(mega_kernel, levels),
        out_shape=(
            jax.ShapeDtypeStruct((tok_rows, width), bf16),
            jax.ShapeDtypeStruct((8, 128), f32),
        ),
        in_specs=[vmem] * 7 + [hbm] * 2,
        out_specs=(vmem, vmem),
        scratch_shapes=[
            pltpu.VMEM((2, chips, rows, half), bf16),
            pltpu.VMEM((2, chips, rows, half), bf16),
            units(chips), units(chips), units(levels), units(levels), units(levels), units(levels),
            pltpu.VMEM((width, 2 * cols), bf16),
            pltpu.VMEM((cols, width), bf16),
            pltpu.VMEM((4 * rows, cols), bf16),
            pltpu.VMEM((tok_rows, width), f32),
            pltpu.VMEM((rows, half), f32),
            pltpu.VMEM((rows, half), f32),
            pltpu.VMEM((tok_rows, width), f32),
            pltpu.VMEM((parts, 8, 128), f32),
            pltpu.VMEM((8, 128), f32),
            dma((2,)), dma, dma,
            dma((levels,)), dma((levels,)), dma((levels,)), dma((levels,)), dma((chips,)), dma((2, chips)),
            dma((chips,)), dma((chips,)), dma((chips,)),
            dma((levels,)), dma((levels,)), dma((levels,)), dma((levels,)), dma, dma,
            dma((parts,)), dma((parts,)),
        ],
        compiler_params=pltpu.CompilerParams(
            collective_id=0, has_side_effects=True, vmem_limit_bytes=60 << 20
        ),
    )(tokens, norm_gain[None, :], mine, live, member, final_gain[None, :], value_head[None, :],
      w_in.reshape(width, 2 * cols), w_down[0])
    return mixed, totals[0, :count] / lengths.astype(f32)


def per_device(reps, parts, *args):
    tokens, w_in, w_down = args[:3]
    tok_rows, width = tokens.shape
    cols = w_in.shape[3]
    row_bytes = 2 * reps * parts * tokens.size * 2
    weight_bytes = 2 * (w_in.size + w_down.size)
    fits = tok_rows % 8 == 0 and width % 1024 == 0 and cols % 256 == 0 and args[7].shape[0] <= 128
    if reps == 2 and parts == 16 and fits and row_bytes < 2 * weight_bytes:
        return mega_rows(reps, parts, *args)
    return move_weights(*args)


def solution(mesh):
    in_specs = (
        P(("rep", "mp"), None),
        P("rep", None, None, "mp"),
        P("rep", "mp", None),
        P(),
        P(),
        P(),
        P("mp"),
        P("rep"),
        P("rep"),
    )
    out_specs = (P(("rep", "mp"), None), P("rep"))
    return jax.shard_map(
        functools.partial(per_device, mesh.shape["rep"], mesh.shape["mp"]),
        mesh=mesh, in_specs=in_specs, out_specs=out_specs, check_vma=False,
    )
```

time: 163 us -> 118 us (0.72)
  matrix products: 29.3 us -> 0 us
  Pallas kernels: 115 us -> 101 us
  other arithmetic: 7.73 us -> 3.44 us
  local copies, waits for them, and re-layouts: 9.79 us -> 12.5 us
    dot_general x2 -> x0, matrix products: 29.3 us -> none  [the longest x1 18.5 us: move_rows(): jnp.dot(rows, w_in.reshape(width, 2 * cols), preferred_element_type=jnp.f...]
    pallas_call x2 -> x1, Pallas kernels: 115 us -> 101 us  [mega_rows(): pl.pallas_call(functools.partial(mega_kernel, levels), out_shape=(jax.Sha...]
    convert_element_type x2 -> x0, other arithmetic: 5.85 us -> none  [the longest x1 4.07 us: move_rows(): jnp.where(mine, jax.nn.gelu(gate, approximate=True) * up, 0.0)]
    unnamed x12 -> x4, local copies, waits for them, and re-layouts: 9.69 us -> 10.6 us
where the time goes in v1:
time: 118 us
  Pallas kernels  101 us (86%)
  local copies, waits for them, and re-layouts  12.5 us (11%)
  other arithmetic  3.44 us (3%)
  between operations  1.31 us (1%)
    pallas_call x1, Pallas kernels, mega_rows(): pl.pallas_call(functools.partial(mega_kernel, levels), out_shape=(jax.Sha...  101 us
    unnamed x4, local copies, waits for them, and re-layouts  10.6 us

profile of v1, /device:TPU:0, one launch (start us, length us, event | category | flops | bytes accessed | tf_op | source)
XLA Modules:
  0.0 118.2 jit_solution(403469897241309830)
XLA Ops:
  1.3 0.7 add.18
  2.0 0.8 fusion
  2.8 0.5 broadcast_in_dim.30.mine_ref
  3.3 0.7 and_convert_fusion
  4.1 0.6 pad.4.member_ref
  4.7 0.7 copy.14.live_ref
  5.4 9.0 %copy.15 = bf16[384,8,2,768]{3,1,2,0:T(8,128)(2,1)} copy(bf16[384,8,2,768]{3,2,1,0:T(2,128)(2,1)} %bitcast.13) | data formatting | bytes 18874368
  14.3 0.0 copy-start
  14.3 101.0 %shard_map.104 = (bf16[40,3072]{1,0:T(8,128)(2,1)}, f32[8,128]{1,0:T(8,128)}) custom-call(bf16[40,3072]{1,0:T(8,128)(2,1)} %tok_ref.1, f32[1,3072]{1,0:T(1,128)} %bitcast.15, f32[1,256]{1,0:T(1,128)} %broadcast_in_dim.30.mine_ref, f32[40,1]{1,0:T(8,128)} %copy.14.live_ref, f32[40,128]{1,0:T(8,128)} %pad.4.member_ref, f32[1,3072]{1,0:T(1,128)} %bitcast.16, ...), custom_call_target="tpu_custom_call" | custom-call | tf_op jit(solution)/shard_map/pallas_call | solution.py:386
  115.3 0.0 copy-done
  115.4 1.2 %bitcast_divide_fusion = f32[8]{0:T(128)} fusion(s32[8]{0:T(128)S(1)} %copy-done, f32[8,128]{1,0:T(8,128)} %get-tuple-element.5), kind=kLoop, calls=%fused_computation.2 | loop fusion | flops 16 | bytes 96 | tf_op jit(solution)/shard_map/div | solution.py:418
  116.6 1.7 %copy.18 = bf16[40,3072]{1,0:T(8,128)(2,1)} copy(bf16[40,3072]{1,0:T(8,128)(2,1)} %get-tuple-element.8) | data formatting | bytes 491520
  (1 shorter events, 0.0 us)
Async XLA Ops:
  14.3 101.0 %copy-start = (s32[8]{0:T(128)S(1)}, s32[8]{0:T(128)}, u32[]{:S(2)}) copy-start(s32[8]{0:T(128)} %param.16) | copy-start | bytes 100

commit v2 on v1

v2 whole, which is shorter than its diff:
```python
import functools

import jax
import jax.numpy as jnp
from jax import lax
from jax.experimental import pallas as pl
from jax.experimental.pallas import tpu as pltpu
from jax.sharding import PartitionSpec as P


def spread(value, axis, source):
    kept = jnp.where(lax.axis_index(axis) == source, value, 0).astype(value.dtype)
    return lax.psum(kept, axis)


def membership(slots, lengths, offsets):
    inside = (slots[:, None] >= offsets[None, :]) & (
        slots[:, None] < offsets[None, :] + lengths[None, :]
    )
    return inside.astype(jnp.float32)


def norm_rows(tokens_f, norm_gain):
    return (
        tokens_f
        * lax.rsqrt(jnp.mean(tokens_f * tokens_f, axis=1, keepdims=True) + 1e-06)
        * norm_gain
    ).astype(jnp.bfloat16)


def finish(tokens_f, delta, final_gain, value_head, lengths, offsets):
    tok_rows = tokens_f.shape[0]
    resid = tokens_f + delta
    mixed = resid.astype(jnp.bfloat16)
    final = resid * lax.rsqrt(jnp.mean(resid * resid, axis=1, keepdims=True) + 1e-06) * final_gain
    values = jnp.dot(final, value_head, precision=lax.Precision.HIGHEST)
    own_slots = lax.axis_index("mp") * tok_rows + jnp.arange(tok_rows, dtype=jnp.int32)
    member = membership(own_slots, lengths, offsets)
    partial_sums = jnp.dot(values, member, precision=lax.Precision.HIGHEST)
    totals = lax.psum(partial_sums, "mp")
    rewards = totals / lengths.astype(jnp.float32)
    return (mixed, rewards)


def move_weights(tokens, w_in, w_down, norm_gain, final_gain, value_head, owner, lengths, offsets):
    owner_index = owner[0]
    width = tokens.shape[1]
    hidden_cols = w_in.shape[3]
    tokens_f = tokens.astype(jnp.float32)
    normed = norm_rows(tokens_f, norm_gain)
    inner_local, outer_local = (
        spread(w_in, "rep", owner_index),
        spread(w_down, "rep", owner_index),
    )
    inner_matrix = inner_local.reshape(width, 2 * hidden_cols)
    piece = lax.all_gather(normed, "mp", axis=0, tiled=True)
    slots = jnp.arange(piece.shape[0], dtype=jnp.int32)
    row_count = piece.shape[0]
    products = jnp.dot(piece, inner_matrix, preferred_element_type=jnp.float32).reshape(
        row_count, 2, hidden_cols
    )
    gate_part = products[:, 0, :]
    up_part = products[:, 1, :]
    hidden = (
        jax.nn.gelu(gate_part, approximate=True)
        * up_part
        * jnp.sum(membership(slots, lengths, offsets), axis=1)[:, None]
    ).astype(jnp.bfloat16)
    outer_matrix = outer_local.reshape(hidden_cols, width)
    delta = lax.psum_scatter(
        jnp.dot(hidden, outer_matrix, preferred_element_type=jnp.float32),
        "mp",
        scatter_dimension=0,
        tiled=True,
    )
    return finish(tokens_f, delta, final_gain, value_head, lengths, offsets)


MESH = pl.DeviceIdType.MESH


def mega_kernel(levels, cuts, tok_ref, gain_ref, final_ref, head_ref, owner_ref, lengths_ref, offsets_ref, win_ref,
                wdown_ref, mixed_ref, rewards_ref,
                x_buf, part, swap_buf, cross_buf, first_buf, second_buf, level_buf, raw, win, wdown, hid,
                acc, mean_buf, own_mean,
                w_sem, up_send, down_send, first_send, second_send, pass_send, recv_sem,
                swap_send, swap_recv, sum_send, cross_recv, first_recv, second_recv, level_recv,
                mean_send, mean_recv):
    rep, slot = lax.axis_index("rep"), lax.axis_index("mp")
    side, row, level = slot % 2, (slot // 2) % 2, slot // 4
    parts = levels * 4
    other_rep, other_row, twin = 1 - rep, 1 - row, 1 - side
    here, cross = (rep, row), (other_rep, other_row)
    first = (rep * side + other_rep * twin, row * twin + other_row * side)
    second = (rep * twin + other_rep * side, row * side + other_row * twin)
    tok_rows, width = tok_ref.shape
    cols, count = wdown.shape[0], lengths_ref.shape[1]
    cut = width // cuts

    def index_of(column, at):
        return at * 4 + column[0] * 2 + column[1]

    def remote(src, dst, send_sem, recv_sem, column, at, plane):
        return pltpu.make_async_remote_copy(
            src_ref=src, dst_ref=dst, send_sem=send_sem, recv_sem=recv_sem,
            device_id=(column[0], at * 4 + column[1] * 2 + plane), device_id_type=MESH,
        )

    barrier = pltpu.get_barrier_semaphore()
    pl.semaphore_signal(barrier, inc=1, device_id=(other_rep, slot), device_id_type=MESH)
    pl.semaphore_signal(barrier, inc=1, device_id=(rep, level * 4 + other_row * 2 + side), device_id_type=MESH)
    pl.semaphore_signal(barrier, inc=1, device_id=(rep, level * 4 + row * 2 + twin), device_id_type=MESH)

    @pl.loop(1, levels)
    def _(d):
        pl.semaphore_signal(barrier, inc=1, device_id=(rep, (slot + 4 * d) % parts), device_id_type=MESH)

    shares = 3
    share = width // shares

    def load_in(i):
        at = pl.ds(i * share, share)
        return pltpu.make_async_copy(win_ref.at[at], raw.at[at], w_sem.at[i])

    load_down = pltpu.make_async_copy(wdown_ref, wdown, w_sem.at[shares])
    for i in range(shares):
        load_in(i).start()
    load_down.start()

    block = 128

    def untangle(i):
        load_in(i).wait()
        to = lax.broadcasted_iota(jnp.int32, (2 * block, 2 * block), 0)
        at = lax.broadcasted_iota(jnp.int32, (2 * block, 2 * block), 1)
        pick = jnp.where((at == 2 * to) | (at == 2 * (to - block) + 1), 1.0, 0.0).astype(jnp.bfloat16)

        @pl.loop(0, share // block, unroll=2)
        def _(k):
            rows_at = pl.ds(pl.multiple_of(i * share + k * block, block), block)
            both_parts = jnp.dot(
                pick, raw[rows_at].reshape(2 * block, cols), preferred_element_type=jnp.float32
            ).astype(jnp.bfloat16)
            win[rows_at, :cols] = both_parts[:block]
            win[rows_at, cols:] = both_parts[block:]

    mine = index_of(here, level)
    tok = tok_ref[...].astype(jnp.float32)
    x_buf[mine, side] = (
        tok * lax.rsqrt(jnp.mean(tok * tok, axis=1, keepdims=True) + 1e-06) * gain_ref[...]
    ).astype(jnp.bfloat16)

    low = level < levels // 2
    inner = (level > 0) & (level < levels - 1)
    outer = jnp.logical_not(inner)

    def from_level(d):
        near = jnp.where(inner & (d < 2), 1 - d, d)
        return jnp.where(low, near, levels - 1 - near)

    def piece(index):
        return x_buf.at[index, side]

    def move(index, sem, column, at):
        return remote(piece(index), piece(index), sem, recv_sem.at[side, index], column, at, side)

    def hand(index):
        return remote(piece(index), piece(index), pass_send.at[index], recv_sem.at[side, index], here, level, twin)

    def arrive(plane, index):
        pltpu.make_async_copy(x_buf.at[index, plane], x_buf.at[index, plane], recv_sem.at[plane, index]).wait()

    def pass_on(index, upward, downward):
        @pl.when(upward & (level < levels - 1))
        def _():
            move(index, up_send.at[index], here, level + 1).start()

        @pl.when(downward & (level > 0))
        def _():
            move(index, down_send.at[index], here, level - 1).start()

        move(index, second_send.at[index], second, level).start()
        hand(index).start()

    def take(column, d):
        at = from_level(d)
        index = index_of(column, at)
        arrive(side, index)
        pass_on(index, at <= level, at >= level)

    def take_level(d):
        take(here, d)
        take(first, d)

    def settle(d):
        for column in (second, cross):
            index = index_of(column, from_level(d))
            arrive(side, index)
            hand(index).start()

    def collect_hands(d):
        for column in (here, first, second, cross):
            arrive(twin, index_of(column, from_level(d)))

    up_block = 256

    def up(d, n):
        lo = n * up_block
        left = x_buf[pl.ds(from_level(d) * 4, 4)].reshape(8 * tok_rows, width)
        gate = jnp.dot(left, win[:, lo:lo + up_block], preferred_element_type=jnp.float32)
        lift = jnp.dot(left, win[:, cols + lo:cols + lo + up_block], preferred_element_type=jnp.float32)
        chosen = jnp.where(owner_ref[...] == rep, 1.0, 0.0)
        hid[:, lo:lo + up_block] = (jax.nn.gelu(gate, approximate=True) * lift * chosen).astype(jnp.bfloat16)

    down_block = 512

    def down(d, q):
        at = from_level(d)

        @pl.loop(0, cut // down_block)
        def _(n):
            lo = pl.multiple_of(n * down_block, down_block)
            out = jnp.dot(hid[...], wdown[:, pl.ds(q * cut + lo, down_block)], preferred_element_type=jnp.float32)
            part[q, pl.ds(at * 4, 4), :, :, pl.ds(lo, down_block)] = out.astype(jnp.bfloat16).reshape(
                4, 2, tok_rows, down_block)

        for column in (cross, second, first, here):
            swap(index_of(column, at), q).start()

    def swap(index, q):
        return remote(part.at[q, index, twin], swap_buf.at[q, index], swap_send.at[q, index],
                      swap_recv.at[q, index], here, level, twin)

    def send(index, q, buf, sem, at, column, to):
        return remote(swap_buf.at[q, index], buf.at[q, at], sum_send.at[q, index], sem.at[q, at], column, to, side)

    def landed(buf, sem, q, at):
        pltpu.make_async_copy(buf.at[q, at], buf.at[q, at], sem.at[q, at]).wait()

    def both(index, q):
        swap(index, q).wait_recv()
        return part[q, index, side].astype(jnp.float32) + swap_buf[q, index].astype(jnp.float32)

    def reduce_outer(d, q, column, buf, sem):
        at = from_level(d)
        index = index_of(column, at)
        swap_buf[q, index] = both(index, q).astype(jnp.bfloat16)
        send(index, q, buf, sem, at, second, level).start()

    def reduce_cross(d, q):
        reduce_outer(d, q, cross, cross_buf, cross_recv)

    def reduce_second(d, q):
        reduce_outer(d, q, second, second_buf, second_recv)

    def reduce_first(d, q):
        at = from_level(d)
        index = index_of(first, at)
        total = both(index, q)
        landed(cross_buf, cross_recv, q, at)
        swap_buf[q, index] = (total + cross_buf[q, at].astype(jnp.float32)).astype(jnp.bfloat16)
        send(index, q, first_buf, first_recv, at, first, level).start()

    def reduce_here(d, q):
        at = from_level(d)
        index = index_of(here, at)
        total = both(index, q)
        landed(second_buf, second_recv, q, at)
        landed(first_buf, first_recv, q, at)
        total = total + (second_buf[q, at].astype(jnp.float32) + first_buf[q, at].astype(jnp.float32))
        if d == 0:
            acc[:, q * cut:(q + 1) * cut] = total
        else:
            swap_buf[q, index] = total.astype(jnp.bfloat16)
            send(index, q, level_buf, level_recv, level, here, at).start()

    pl.semaphore_wait(barrier, 3 + levels - 1)
    always = level >= 0
    move(mine, first_send, first, level).start()
    pass_on(mine, always, always)
    for i in range(shares):
        untangle(i)

    take(first, 0)
    take_level(1)

    @pl.when(inner)
    def _():
        take_level(2)

    settle(0)
    collect_hands(0)
    load_down.wait()

    def all_cuts(step, d):
        for q in range(cuts):
            step(d, q)

    ups = cols // up_block

    def up_all(d, lo=0, hi=ups):
        for n in range(lo, hi):
            up(d, n)

    def down_all(d):
        all_cuts(down, d)

    up_all(0, 0, 2)

    @pl.when(inner)
    def _():
        take(here, 3)

    up_all(0, 2)

    @pl.when(inner)
    def _():
        take(first, 3)

    down_all(0)
    all_cuts(reduce_cross, 0)
    all_cuts(reduce_second, 0)
    settle(1)
    collect_hands(1)
    up_all(1, 0, 1)

    @pl.when(outer)
    def _():
        take(here, 2)

    up_all(1, 1)
    all_cuts(reduce_first, 0)
    down(1, 0)

    @pl.when(outer)
    def _():
        take(first, 2)

    for q in range(1, cuts):
        down(1, q)
    all_cuts(reduce_cross, 1)
    all_cuts(reduce_second, 1)
    all_cuts(reduce_here, 0)

    @pl.when(outer)
    def _():
        take(here, 3)

    settle(2)
    collect_hands(2)
    up_all(2)
    all_cuts(reduce_first, 1)

    @pl.when(outer)
    def _():
        take(first, 3)

    down_all(2)
    all_cuts(reduce_cross, 2)
    all_cuts(reduce_second, 2)
    all_cuts(reduce_here, 1)
    settle(3)
    collect_hands(3)
    up_all(3)
    all_cuts(reduce_first, 2)
    down_all(3)
    all_cuts(reduce_cross, 3)
    all_cuts(reduce_second, 3)
    all_cuts(reduce_here, 2)
    all_cuts(reduce_first, 3)
    all_cuts(reduce_here, 3)

    for q in range(cuts):
        @pl.loop(1, levels)
        def _(d):
            at = (level + d) % levels
            landed(level_buf, level_recv, q, at)
            acc[:, q * cut:(q + 1) * cut] += level_buf[q, at].astype(jnp.float32)

    own_slots = slot * tok_rows + lax.broadcasted_iota(jnp.int32, (tok_rows, count), 0)
    starts = offsets_ref[...]
    member = jnp.where((own_slots >= starts) & (own_slots < starts + lengths_ref[...]), 1.0, 0.0)
    live = jnp.sum(member, axis=1, keepdims=True)
    resid = tok_ref[...].astype(jnp.float32) + acc[...] * live
    scale = lax.rsqrt(jnp.mean(resid * resid, axis=1, keepdims=True) + 1e-06)
    values = jnp.sum(resid * scale * final_ref[...] * head_ref[...], axis=1, keepdims=True)
    own_mean[...] = jnp.broadcast_to(jnp.sum(values * member, axis=0, keepdims=True), own_mean.shape)

    def tell(d):
        to = (slot + d) % parts
        return pltpu.make_async_remote_copy(
            src_ref=own_mean, dst_ref=mean_buf.at[slot], send_sem=mean_send.at[to],
            recv_sem=mean_recv.at[slot], device_id=(rep, to), device_id_type=MESH,
        )

    @pl.loop(1, parts)
    def _(d):
        tell(d).start()

    mixed_ref[...] = resid.astype(jnp.bfloat16)
    acc[:8, :count] = own_mean[...]
    move(mine, first_send, first, level).wait_send()

    @pl.loop(0, levels)
    def _(d):
        for column in (here, first):
            index = index_of(column, d)
            move(index, second_send.at[index], second, level).wait_send()

            @pl.when((d <= level) & (level < levels - 1))
            def _():
                move(index, up_send.at[index], here, level).wait_send()

            @pl.when((d >= level) & (level > 0))
            def _():
                move(index, down_send.at[index], here, level).wait_send()

    @pl.loop(0, parts)
    def _(i):
        hand(i).wait_send()
        for q in range(cuts):
            swap(i, q).wait_send()

    @pl.loop(0, levels)
    def _(d):
        for q in range(cuts):
            for column in (cross, second, first):
                send(index_of(column, d), q, cross_buf, cross_recv, level, second, level).wait_send()

    @pl.loop(1, levels)
    def _(d):
        for q in range(cuts):
            send(index_of(here, (level + d) % levels), q, level_buf, level_recv, level, second, level).wait_send()

    @pl.loop(1, parts)
    def _(d):
        index = (slot + parts - d) % parts
        pltpu.make_async_copy(own_mean, mean_buf.at[index], mean_recv.at[index]).wait()
        acc[:8, :count] += mean_buf[index]

    rewards_ref[...] = acc[:1, :count] / lengths_ref[...].astype(jnp.float32)

    @pl.loop(1, parts)
    def _(d):
        tell(d).wait_send()


def mega_rows(reps, parts, tokens, w_in, w_down, norm_gain, final_gain, value_head, owner, lengths, offsets):
    tok_rows, width = tokens.shape
    cols = w_in.shape[3]
    levels, cuts = parts // 4, 2
    cut, count = width // cuts, lengths.shape[0]
    vmem = pl.BlockSpec(memory_space=pltpu.VMEM)
    hbm = pl.BlockSpec(memory_space=pl.ANY)
    dma = pltpu.SemaphoreType.DMA
    f32, bf16 = jnp.float32, jnp.bfloat16
    few = pltpu.VMEM((cuts, levels, tok_rows, cut), bf16)
    some, each = dma((cuts, levels)), dma((cuts, parts))
    mixed, rewards = pl.pallas_call(
        functools.partial(mega_kernel, levels, cuts),
        out_shape=(
            jax.ShapeDtypeStruct((tok_rows, width), bf16),
            jax.ShapeDtypeStruct((1, count), f32),
        ),
        in_specs=[vmem] * 7 + [hbm] * 2,
        out_specs=(vmem, vmem),
        scratch_shapes=[
            pltpu.VMEM((parts, 2, tok_rows, width), bf16),
            pltpu.VMEM((cuts, parts, 2, tok_rows, cut), bf16),
            pltpu.VMEM((cuts, parts, tok_rows, cut), bf16),
            few, few, few, few,
            pltpu.VMEM((width, 2, cols), bf16),
            pltpu.VMEM((width, 2 * cols), bf16),
            pltpu.VMEM((cols, width), bf16),
            pltpu.VMEM((8 * tok_rows, cols), bf16),
            pltpu.VMEM((tok_rows, width), f32),
            pltpu.VMEM((parts, 8, count), f32),
            pltpu.VMEM((8, count), f32),
            dma((4,)), dma((parts,)), dma((parts,)), dma, dma((parts,)), dma((parts,)), dma((2, parts)),
            each, each, each, some, some, some, some,
            dma((parts,)), dma((parts,)),
        ],
        compiler_params=pltpu.CompilerParams(
            collective_id=0, has_side_effects=True, vmem_limit_bytes=54 << 20
        ),
    )(tokens, norm_gain[None, :], final_gain[None, :], value_head[None, :], owner[None, :], lengths[None, :],
      offsets[None, :], w_in[0], w_down[0])
    return mixed, rewards[0]


def per_device(reps, parts, *args):
    tokens, w_in, w_down = args[:3]
    tok_rows, width = tokens.shape
    cols = w_in.shape[3]
    row_bytes = 2 * reps * parts * tokens.size * 2
    weight_bytes = 2 * (w_in.size + w_down.size)
    fits = tok_rows % 8 == 0 and width % 3072 == 0 and cols % 256 == 0 and args[7].shape[0] <= 128
    if reps == 2 and parts == 16 and fits and row_bytes < 2 * weight_bytes:
        return mega_rows(reps, parts, *args)
    return move_weights(*args)


def solution(mesh):
    in_specs = (
        P(("rep", "mp"), None),
        P("rep", None, None, "mp"),
        P("rep", "mp", None),
        P(),
        P(),
        P(),
        P("mp"),
        P("rep"),
        P("rep"),
    )
    out_specs = (P(("rep", "mp"), None), P("rep"))
    return jax.shard_map(
        functools.partial(per_device, mesh.shape["rep"], mesh.shape["mp"]),
        mesh=mesh, in_specs=in_specs, out_specs=out_specs, check_vma=False,
    )
```

time: 118 us -> 99.1 us (0.84)
  local copies, waits for them, and re-layouts: 12.5 us -> 2.83 us
  Pallas kernels: 101 us -> 94.8 us
  other arithmetic: 3.44 us -> 0 us
    unnamed x4 -> x2, local copies, waits for them, and re-layouts: 10.6 us -> 2.83 us
    pallas_call x1, Pallas kernels: 101 us -> 94.8 us  [mega_rows(): pl.pallas_call(functools.partial(mega_kernel, levels, cuts), out_shape=(j...]
    broadcast_in_dim x2 -> x0, local copies, waits for them, and re-layouts: 1.24 us -> none  [the longest x1 0.69 us: mega_rows(): live = jnp.sum(member, axis=1)[:, None]]
    div x1 -> x0, other arithmetic: 1.2 us -> none  [mega_rows(): return (mixed, totals[0, :count] / lengths.astype(f32))]
where the time goes in v2:
time: 99.1 us; the launch traced here: 99 us
  Pallas kernels  94.8 us (96%)
  local copies, waits for them, and re-layouts  2.83 us (3%)
  between operations  1.29 us (1%)
    pallas_call x1, Pallas kernels, mega_rows(): pl.pallas_call(functools.partial(mega_kernel, levels, cuts), out_shape=(j...  94.8 us
    unnamed x2, local copies, waits for them, and re-layouts  2.83 us

profile of v2, /device:TPU:0, one launch (start us, length us, event | category | flops | bytes accessed | tf_op | source)
XLA Modules:
  0.0 99.0 jit_solution(12073722196835423382)
XLA Ops:
  1.3 94.8 %shard_map.104 = (bf16[40,3072]{1,0:T(8,128)(2,1)}, f32[1,8]{1,0:T(1,128)}) custom-call(bf16[40,3072]{1,0:T(8,128)(2,1)} %tok_ref.1, f32[1,3072]{1,0:T(1,128)} %bitcast.12, f32[1,3072]{1,0:T(1,128)} %bitcast.13, f32[1,3072]{1,0:T(1,128)} %bitcast.14, s32[1,1]{1,0:T(1,128)} %bitcast.9.owner_ref, s32[1,8]{1,0:T(1,128)} %bitcast.15, s32[1,8]{1,0:T(1,128)} %bitcast.16, ...), custom_call_target="tpu_custom_call" | custom-call | tf_op jit(solution)/shard_map/pallas_call | solution.py:459
  96.1 1.7 %copy.14 = bf16[40,3072]{1,0:T(8,128)(2,1)} copy(bf16[40,3072]{1,0:T(8,128)(2,1)} %get-tuple-element.8) | data formatting | bytes 491520
  97.8 1.2 %copy.15 = f32[8]{0:T(128)} copy(f32[8]{0:T(128)} %bitcast.17) | data formatting | bytes 64

commit v3 on v2

--- a/solution.py
+++ b/solution.py
@@ -79,7 +79,7 @@
 MESH = pl.DeviceIdType.MESH
 
 
-def mega_kernel(levels, cuts, tok_ref, gain_ref, final_ref, head_ref, owner_ref, lengths_ref, offsets_ref, win_ref,
+def mega_kernel(levels, cuts, slices, tok_ref, gain_ref, final_ref, head_ref, owner_ref, lengths_ref, offsets_ref, win_ref,
                 wdown_ref, mixed_ref, rewards_ref,
                 x_buf, part, swap_buf, cross_buf, first_buf, second_buf, level_buf, raw, win, wdown, hid,
                 acc, mean_buf, own_mean,
@@ -96,6 +96,7 @@
     tok_rows, width = tok_ref.shape
     cols, count = wdown.shape[0], lengths_ref.shape[1]
     cut = width // cuts
+    slab = width // slices
 
     def index_of(column, at):
         return at * 4 + column[0] * 2 + column[1]
@@ -155,52 +156,51 @@
     outer = jnp.logical_not(inner)
 
     def from_level(d):
-        near = jnp.where(inner & (d < 2), 1 - d, d)
+        near = jnp.where(inner, (1, 0, 2, 3)[d], d)
         return jnp.where(low, near, levels - 1 - near)
 
-    def piece(index):
-        return x_buf.at[index, side]
-
-    def move(index, sem, column, at):
-        return remote(piece(index), piece(index), sem, recv_sem.at[side, index], column, at, side)
-
-    def hand(index):
-        return remote(piece(index), piece(index), pass_send.at[index], recv_sem.at[side, index], here, level, twin)
-
-    def arrive(plane, index):
-        pltpu.make_async_copy(x_buf.at[index, plane], x_buf.at[index, plane], recv_sem.at[plane, index]).wait()
-
-    def pass_on(index, upward, downward):
+    def piece(index, plane, s):
+        return x_buf.at[index, plane, :, pl.ds(s * slab, slab)]
+
+    def move(index, s, sem, column, at):
+        return remote(piece(index, side, s), piece(index, side, s), sem.at[index, s], recv_sem.at[side, index, s],
+                      column, at, side)
+
+    def hand(index, s):
+        return remote(piece(index, side, s), piece(index, side, s), pass_send.at[index, s],
+                      recv_sem.at[side, index, s], here, level, twin)
+
+    def arrive(plane, index, s):
+        at = piece(index, plane, s)
+        pltpu.make_async_copy(at, at, recv_sem.at[plane, index, s]).wait()
+
+    def pass_on(index, s, upward, downward):
         @pl.when(upward & (level < levels - 1))
         def _():
-            move(index, up_send.at[index], here, level + 1).start()
+            move(index, s, up_send, here, level + 1).start()
 
         @pl.when(downward & (level > 0))
         def _():
-            move(index, down_send.at[index], here, level - 1).start()
-
-        move(index, second_send.at[index], second, level).start()
-        hand(index).start()
-
-    def take(column, d):
+            move(index, s, down_send, here, level - 1).start()
+
+        move(index, s, second_send, second, level).start()
+        hand(index, s).start()
+
+    def take(column, d, s):
         at = from_level(d)
         index = index_of(column, at)
-        arrive(side, index)
-        pass_on(index, at <= level, at >= level)
-
-    def take_level(d):
-        take(here, d)
-        take(first, d)
-
-    def settle(d):
-        for column in (second, cross):
-            index = index_of(column, from_level(d))
-            arrive(side, index)
-            hand(index).start()
+        arrive(side, index, s)
+        pass_on(index, s, at <= level, at >= level)
+
+    def settle(column, d, s):
+        index = index_of(column, from_level(d))
+        arrive(side, index, s)
+        hand(index, s).start()
 
     def collect_hands(d):
         for column in (here, first, second, cross):
-            arrive(twin, index_of(column, from_level(d)))
+            for s in range(slices):
+                arrive(twin, index_of(column, from_level(d)), s)
 
     up_block = 256
 
@@ -276,99 +276,165 @@
 
     pl.semaphore_wait(barrier, 3 + levels - 1)
     always = level >= 0
-    move(mine, first_send, first, level).start()
-    pass_on(mine, always, always)
-    for i in range(shares):
-        untangle(i)
-
-    take(first, 0)
-    take_level(1)
-
-    @pl.when(inner)
-    def _():
-        take_level(2)
-
-    settle(0)
+    for s in range(slices):
+        move(mine, s, first_send, first, level).start()
+        pass_on(mine, s, always, always)
+    untangle(0)
+    untangle(1)
+    untangle(2)
+    take(first, 0, 0)
+
+    @pl.when(inner)
+    def _():
+        take(here, 1, 0)
+
+    @pl.when(outer)
+    def _():
+        take(here, 1, 0)
+    settle(second, 0, 0)
+
+    @pl.when(inner)
+    def _():
+        take(here, 2, 0)
+    settle(cross, 0, 0)
     collect_hands(0)
+    up(0, 0)
+
+    @pl.when(inner)
+    def _():
+        take(first, 1, 0)
+
+    @pl.when(outer)
+    def _():
+        take(first, 1, 0)
+
+    @pl.when(inner)
+    def _():
+        settle(second, 1, 0)
+
+    @pl.when(outer)
+    def _():
+        settle(second, 1, 0)
+
+    @pl.when(inner)
+    def _():
+        take(first, 2, 0)
+    up(0, 1)
+    up(0, 2)
     load_down.wait()
-
-    def all_cuts(step, d):
-        for q in range(cuts):
-            step(d, q)
-
-    ups = cols // up_block
-
-    def up_all(d, lo=0, hi=ups):
-        for n in range(lo, hi):
-            up(d, n)
-
-    def down_all(d):
-        all_cuts(down, d)
-
-    up_all(0, 0, 2)
-
-    @pl.when(inner)
-    def _():
-        take(here, 3)
-
-    up_all(0, 2)
-
-    @pl.when(inner)
-    def _():
-        take(first, 3)
-
-    down_all(0)
-    all_cuts(reduce_cross, 0)
-    all_cuts(reduce_second, 0)
-    settle(1)
+    down(0, 0)
+
+    @pl.when(inner)
+    def _():
+        settle(cross, 1, 0)
+
+    @pl.when(outer)
+    def _():
+        settle(cross, 1, 0)
+    reduce_cross(0, 0)
+
+    @pl.when(inner)
+    def _():
+        take(here, 3, 0)
+    down(0, 1)
     collect_hands(1)
-    up_all(1, 0, 1)
-
-    @pl.when(outer)
-    def _():
-        take(here, 2)
-
-    up_all(1, 1)
-    all_cuts(reduce_first, 0)
+    reduce_second(0, 0)
+
+    @pl.when(outer)
+    def _():
+        take(here, 2, 0)
+        take(first, 2, 0)
+    up(1, 0)
+
+    @pl.when(inner)
+    def _():
+        settle(second, 2, 0)
+
+    @pl.when(outer)
+    def _():
+        settle(second, 2, 0)
+    reduce_cross(0, 1)
+    up(1, 1)
+    reduce_second(0, 1)
+    up(1, 2)
     down(1, 0)
 
     @pl.when(outer)
     def _():
-        take(first, 2)
-
-    for q in range(1, cuts):
-        down(1, q)
-    all_cuts(reduce_cross, 1)
-    all_cuts(reduce_second, 1)
-    all_cuts(reduce_here, 0)
-
-    @pl.when(outer)
-    def _():
-        take(here, 3)
-
-    settle(2)
+        take(here, 3, 0)
+    down(1, 1)
+
+    @pl.when(inner)
+    def _():
+        settle(cross, 2, 0)
+
+    @pl.when(outer)
+    def _():
+        settle(cross, 2, 0)
+    reduce_second(1, 0)
+    reduce_second(1, 1)
+    reduce_cross(1, 1)
+
+    @pl.when(inner)
+    def _():
+        take(first, 3, 0)
     collect_hands(2)
-    up_all(2)
-    all_cuts(reduce_first, 1)
-
-    @pl.when(outer)
-    def _():
-        take(first, 3)
-
-    down_all(2)
-    all_cuts(reduce_cross, 2)
-    all_cuts(reduce_second, 2)
-    all_cuts(reduce_here, 1)
-    settle(3)
+    up(2, 0)
+    up(2, 1)
+
+    @pl.when(outer)
+    def _():
+        take(first, 3, 0)
+
+    @pl.when(inner)
+    def _():
+        settle(second, 3, 0)
+
+    @pl.when(outer)
+    def _():
+        settle(second, 3, 0)
+    up(2, 2)
+    reduce_cross(1, 0)
+    down(2, 0)
+    down(2, 1)
+    reduce_cross(2, 0)
+    reduce_second(2, 0)
+    reduce_cross(2, 1)
+
+    @pl.when(inner)
+    def _():
+        settle(cross, 3, 0)
+
+    @pl.when(outer)
+    def _():
+        settle(cross, 3, 0)
     collect_hands(3)
-    up_all(3)
-    all_cuts(reduce_first, 2)
-    down_all(3)
-    all_cuts(reduce_cross, 3)
-    all_cuts(reduce_second, 3)
-    all_cuts(reduce_here, 2)
-    all_cuts(reduce_first, 3)
-    all_cuts(reduce_here, 3)
+    up(3, 0)
+    reduce_first(2, 0)
+    reduce_second(2, 1)
+    up(3, 1)
+    reduce_first(2, 1)
+    up(3, 2)
+    reduce_first(1, 1)
+    reduce_first(1, 0)
+    reduce_here(2, 0)
+    down(3, 0)
+    reduce_cross(3, 0)
+    reduce_here(2, 1)
+    down(3, 1)
+    reduce_second(3, 0)
+    reduce_cross(3, 1)
+    reduce_here(1, 1)
+    reduce_here(1, 0)
+    reduce_second(3, 1)
+    reduce_first(3, 0)
+    reduce_first(3, 1)
+    reduce_here(3, 0)
+    reduce_first(0, 0)
+    reduce_first(0, 1)
+    reduce_here(3, 1)
+    reduce_here(0, 1)
+    reduce_here(0, 0)
 
     for q in range(cuts):
         @pl.loop(1, levels)
@@ -399,25 +465,28 @@
 
     mixed_ref[...] = resid.astype(jnp.bfloat16)
     acc[:8, :count] = own_mean[...]
-    move(mine, first_send, first, level).wait_send()
-
-    @pl.loop(0, levels)
-    def _(d):
-        for column in (here, first):
-            index = index_of(column, d)
-            move(index, second_send.at[index], second, level).wait_send()
-
-            @pl.when((d <= level) & (level < levels - 1))
-            def _():
-                move(index, up_send.at[index], here, level).wait_send()
-
-            @pl.when((d >= level) & (level > 0))
-            def _():
-                move(index, down_send.at[index], here, level).wait_send()
+    @pl.loop(0, slices)
+    def _(s):
+        move(mine, s, first_send, first, level).wait_send()
+
+        @pl.loop(0, levels)
+        def _(d):
+            for column in (here, first):
+                index = index_of(column, d)
+                move(index, s, second_send, second, level).wait_send()
+
+                @pl.when((d <= level) & (level < levels - 1))
+                def _():
+                    move(index, s, up_send, here, level).wait_send()
+
+                @pl.when((d >= level) & (level > 0))
+                def _():
+                    move(index, s, down_send, here, level).wait_send()
 
     @pl.loop(0, parts)
     def _(i):
-        hand(i).wait_send()
+        for s in range(slices):
+            hand(i, s).wait_send()
         for q in range(cuts):
             swap(i, q).wait_send()
 
@@ -448,16 +517,16 @@
 def mega_rows(reps, parts, tokens, w_in, w_down, norm_gain, final_gain, value_head, owner, lengths, offsets):
     tok_rows, width = tokens.shape
     cols = w_in.shape[3]
-    levels, cuts = parts // 4, 2
+    levels, cuts, slices = parts // 4, 2, 1
     cut, count = width // cuts, lengths.shape[0]
     vmem = pl.BlockSpec(memory_space=pltpu.VMEM)
     hbm = pl.BlockSpec(memory_space=pl.ANY)
     dma = pltpu.SemaphoreType.DMA
     f32, bf16 = jnp.float32, jnp.bfloat16
     few = pltpu.VMEM((cuts, levels, tok_rows, cut), bf16)
-    some, each = dma((cuts, levels)), dma((cuts, parts))
+    some, each, hop = dma((cuts, levels)), dma((cuts, parts)), dma((parts, slices))
     mixed, rewards = pl.pallas_call(
-        functools.partial(mega_kernel, levels, cuts),
+        functools.partial(mega_kernel, levels, cuts, slices),
         out_shape=(
             jax.ShapeDtypeStruct((tok_rows, width), bf16),
             jax.ShapeDtypeStruct((1, count), f32),
@@ -476,12 +545,12 @@
             pltpu.VMEM((tok_rows, width), f32),
             pltpu.VMEM((parts, 8, count), f32),
             pltpu.VMEM((8, count), f32),
-            dma((4,)), dma((parts,)), dma((parts,)), dma, dma((parts,)), dma((parts,)), dma((2, parts)),
+            dma((4,)), hop, hop, hop, hop, hop, dma((2, parts, slices)),
             each, each, each, some, some, some, some,
             dma((parts,)), dma((parts,)),
         ],
         compiler_params=pltpu.CompilerParams(
-            collective_id=0, has_side_effects=True, vmem_limit_bytes=54 << 20
+            collective_id=0, has_side_effects=True, vmem_limit_bytes=53477376
         ),
     )(tokens, norm_gain[None, :], final_gain[None, :], value_head[None, :], owner[None, :], lengths[None, :],
       offsets[None, :], w_in[0], w_down[0])

time: 99.1 us -> 90.1 us (0.909)
  Pallas kernels: 94.8 us -> 82.8 us
  local copies, waits for them, and re-layouts: 2.83 us -> 5.57 us
    pallas_call x1, Pallas kernels: 94.8 us -> 82.8 us  [mega_rows(): pl.pallas_call(functools.partial(mega_kernel, levels, cuts, slices), out_...]
    unnamed x2 -> x14, local copies, waits for them, and re-layouts: 2.83 us -> 5.57 us
where the time goes in v3:
time: 90.1 us; the launch traced here: 89.7 us
  Pallas kernels  82.8 us (92%)
  local copies, waits for them, and re-layouts  5.57 us (6%)
  between operations  1.3 us (1%)
    pallas_call x1, Pallas kernels, mega_rows(): pl.pallas_call(functools.partial(mega_kernel, levels, cuts, slices), out_...  82.8 us
    unnamed x14, local copies, waits for them, and re-layouts  5.57 us

profile of v3, /device:TPU:0, one launch (start us, length us, event | category | flops | bytes accessed | tf_op | source)
XLA Modules:
  0.0 89.7 jit_solution(14306357070587606559)
XLA Ops:
  1.3 0.0 copy-start
  1.3 0.9 %copy-done = bf16[40,3072]{1,0:T(8,128)(2,1)S(1)} copy-done((bf16[40,3072]{1,0:T(8,128)(2,1)S(1)}, bf16[40,3072]{1,0:T(8,128)(2,1)}, u32[]{:S(2)}) %copy-start) | copy-done | bytes 245784
  2.2 0.0 copy-start.1
  2.2 0.7 copy-done.1
  2.9 0.0 copy-start.2
  2.9 0.7 copy-done.2
  3.6 0.0 copy-start.3
  3.6 0.7 copy-done.3
  4.3 0.0 copy-start.4
  4.3 0.7 copy-done.4
  5.0 0.0 copy-start.5
  5.0 0.7 copy-done.5
  5.7 82.8 %shard_map.104 = (bf16[40,3072]{1,0:T(8,128)(2,1)S(1)}, f32[1,8]{1,0:T(1,128)S(1)}) custom-call(bf16[40,3072]{1,0:T(8,128)(2,1)S(1)} %copy-done, f32[1,3072]{1,0:T(1,128)S(1)} %bitcast.10, f32[1,3072]{1,0:T(1,128)S(1)} %bitcast.11, f32[1,3072]{1,0:T(1,128)S(1)} %bitcast.12, s32[1,1]{1,0:T(1,128)} %bitcast.9.owner_ref, s32[1,8]{1,0:T(1,128)S(1)} %bitcast.13, ...), custom_call_target="tpu_custom_call" | custom-call | tf_op jit(solution)/shard_map/pallas_call | solution.py:528
  88.5 0.7 copy.14
  89.2 0.5 copy.15
Async XLA Ops:
  1.3 0.9 %copy-start = (bf16[40,3072]{1,0:T(8,128)(2,1)S(1)}, bf16[40,3072]{1,0:T(8,128)(2,1)}, u32[]{:S(2)}) copy-start(bf16[40,3072]{1,0:T(8,128)(2,1)} %tok_ref.1) | copy-start | bytes 737284
  2.2 0.7 copy-start.1
  2.9 0.7 copy-start.2
  3.6 0.7 copy-start.3
  4.3 0.7 copy-start.4
  5.0 0.7 copy-start.5

commit v4 on v3

--- a/solution.py
+++ b/solution.py
@@ -81,10 +81,10 @@
 
 def mega_kernel(levels, cuts, slices, tok_ref, gain_ref, final_ref, head_ref, owner_ref, lengths_ref, offsets_ref, win_ref,
                 wdown_ref, mixed_ref, rewards_ref,
-                x_buf, part, swap_buf, cross_buf, first_buf, second_buf, level_buf, raw, win, wdown, hid,
+                x_buf, part, swap_buf, cross_buf, first_buf, second_buf, level_buf, near_buf, raw, win, wdown, hid,
                 acc, mean_buf, own_mean,
                 w_sem, up_send, down_send, first_send, second_send, pass_send, recv_sem,
-                swap_send, swap_recv, sum_send, cross_recv, first_recv, second_recv, level_recv,
+                swap_send, swap_recv, sum_send, cross_recv, first_recv, second_recv, level_recv, near_recv,
                 mean_send, mean_recv):
     rep, slot = lax.axis_index("rep"), lax.axis_index("mp")
     side, row, level = slot % 2, (slot // 2) % 2, slot // 4
@@ -258,16 +258,26 @@
         index = index_of(first, at)
         total = both(index, q)
         landed(cross_buf, cross_recv, q, at)
-        swap_buf[q, index] = (total + cross_buf[q, at].astype(jnp.float32)).astype(jnp.bfloat16)
-        send(index, q, first_buf, first_recv, at, first, level).start()
+        total = total + cross_buf[q, at].astype(jnp.float32)
+        if d == 0:
+            beside = from_level(1)
+            landed(near_buf, near_recv, q, beside)
+            total = total + near_buf[q, beside].astype(jnp.float32)
+        swap_buf[q, index] = total.astype(jnp.bfloat16)
+        if d == 1:
+            send(index, q, near_buf, near_recv, level, here, at).start()
+        else:
+            send(index, q, first_buf, first_recv, at, first, level).start()
 
     def reduce_here(d, q):
         at = from_level(d)
         index = index_of(here, at)
         total = both(index, q)
         landed(second_buf, second_recv, q, at)
-        landed(first_buf, first_recv, q, at)
-        total = total + (second_buf[q, at].astype(jnp.float32) + first_buf[q, at].astype(jnp.float32))
+        total = total + second_buf[q, at].astype(jnp.float32)
+        if d != 1:
+            landed(first_buf, first_recv, q, at)
+            total = total + first_buf[q, at].astype(jnp.float32)
         if d == 0:
             acc[:, q * cut:(q + 1) * cut] = total
         else:
@@ -281,160 +291,148 @@
         pass_on(mine, s, always, always)
     untangle(0)
     untangle(1)
-    untangle(2)
-    take(first, 0, 0)
-
-    @pl.when(inner)
-    def _():
-        take(here, 1, 0)
 
     @pl.when(outer)
     def _():
         take(here, 1, 0)
     settle(second, 0, 0)
+    take(first, 0, 0)
 
     @pl.when(inner)
     def _():
         take(here, 2, 0)
+        take(here, 1, 0)
     settle(cross, 0, 0)
+
+    @pl.when(outer)
+    def _():
+        take(first, 1, 0)
+    untangle(2)
     collect_hands(0)
     up(0, 0)
 
     @pl.when(inner)
     def _():
         take(first, 1, 0)
-
-    @pl.when(outer)
-    def _():
-        take(first, 1, 0)
-
-    @pl.when(inner)
+    up(0, 1)
+
+    @pl.when(inner)
+    def _():
+        take(first, 2, 0)
+    up(0, 2)
+
+    @pl.when(outer)
     def _():
         settle(second, 1, 0)
-
-    @pl.when(outer)
-    def _():
-        settle(second, 1, 0)
-
-    @pl.when(inner)
-    def _():
-        take(first, 2, 0)
-    up(0, 1)
-    up(0, 2)
+        take(here, 2, 0)
+        settle(cross, 1, 0)
     load_down.wait()
     down(0, 0)
+    reduce_cross(0, 0)
 
     @pl.when(inner)
     def _():
         settle(cross, 1, 0)
-
-    @pl.when(outer)
-    def _():
-        settle(cross, 1, 0)
-    reduce_cross(0, 0)
-
-    @pl.when(inner)
-    def _():
+        settle(second, 1, 0)
         take(here, 3, 0)
     down(0, 1)
     collect_hands(1)
-    reduce_second(0, 0)
-
-    @pl.when(outer)
-    def _():
-        take(here, 2, 0)
+
+    @pl.when(outer)
+    def _():
         take(first, 2, 0)
     up(1, 0)
-
-    @pl.when(inner)
+    up(1, 1)
+    up(1, 2)
+
+    @pl.when(outer)
     def _():
         settle(second, 2, 0)
 
-    @pl.when(outer)
+    @pl.when(inner)
+    def _():
+        take(first, 3, 0)
+    reduce_cross(0, 1)
+
+    @pl.when(outer)
+    def _():
+        settle(cross, 2, 0)
+
+    @pl.when(inner)
     def _():
         settle(second, 2, 0)
-    reduce_cross(0, 1)
-    up(1, 1)
-    reduce_second(0, 1)
-    up(1, 2)
+
+    @pl.when(outer)
+    def _():
+        take(here, 3, 0)
+
+    @pl.when(inner)
+    def _():
+        settle(cross, 2, 0)
     down(1, 0)
-
-    @pl.when(outer)
-    def _():
-        take(here, 3, 0)
     down(1, 1)
-
-    @pl.when(inner)
-    def _():
-        settle(cross, 2, 0)
-
-    @pl.when(outer)
-    def _():
-        settle(cross, 2, 0)
+    collect_hands(2)
+    reduce_cross(1, 0)
+    up(2, 0)
+    reduce_cross(1, 1)
+    up(2, 1)
+
+    @pl.when(outer)
+    def _():
+        take(first, 3, 0)
+
+    @pl.when(inner)
+    def _():
+        settle(cross, 3, 0)
+    up(2, 2)
     reduce_second(1, 0)
-    reduce_second(1, 1)
-    reduce_cross(1, 1)
-
-    @pl.when(inner)
-    def _():
-        take(first, 3, 0)
-    collect_hands(2)
-    up(2, 0)
-    up(2, 1)
-
-    @pl.when(outer)
-    def _():
-        take(first, 3, 0)
-
-    @pl.when(inner)
+
+    @pl.when(outer)
     def _():
         settle(second, 3, 0)
-
-    @pl.when(outer)
-    def _():
-        settle(second, 3, 0)
-    up(2, 2)
-    reduce_cross(1, 0)
     down(2, 0)
     down(2, 1)
     reduce_cross(2, 0)
+    reduce_first(1, 1)
+
+    @pl.when(outer)
+    def _():
+        settle(cross, 3, 0)
+    reduce_first(1, 0)
+
+    @pl.when(inner)
+    def _():
+        settle(second, 3, 0)
+    reduce_cross(2, 1)
     reduce_second(2, 0)
-    reduce_cross(2, 1)
-
-    @pl.when(inner)
-    def _():
-        settle(cross, 3, 0)
-
-    @pl.when(outer)
-    def _():
-        settle(cross, 3, 0)
+    reduce_second(2, 1)
     collect_hands(3)
     up(3, 0)
+    reduce_here(1, 0)
     reduce_first(2, 0)
-    reduce_second(2, 1)
     up(3, 1)
+    up(3, 2)
     reduce_first(2, 1)
-    up(3, 2)
-    reduce_first(1, 1)
-    reduce_first(1, 0)
+    down(3, 0)
     reduce_here(2, 0)
-    down(3, 0)
+    reduce_second(1, 1)
     reduce_cross(3, 0)
+    down(3, 1)
     reduce_here(2, 1)
-    down(3, 1)
+    reduce_cross(3, 1)
     reduce_second(3, 0)
-    reduce_cross(3, 1)
-    reduce_here(1, 1)
-    reduce_here(1, 0)
-    reduce_second(3, 1)
     reduce_first(3, 0)
     reduce_first(3, 1)
+    reduce_here(1, 1)
+    reduce_second(3, 1)
+    reduce_second(0, 0)
+    reduce_first(0, 0)
     reduce_here(3, 0)
-    reduce_first(0, 0)
+    reduce_here(3, 1)
+    reduce_second(0, 1)
     reduce_first(0, 1)
-    reduce_here(3, 1)
+    reduce_here(0, 0)
     reduce_here(0, 1)
-    reduce_here(0, 0)
 
     for q in range(cuts):
         @pl.loop(1, levels)
@@ -537,7 +535,7 @@
             pltpu.VMEM((parts, 2, tok_rows, width), bf16),
             pltpu.VMEM((cuts, parts, 2, tok_rows, cut), bf16),
             pltpu.VMEM((cuts, parts, tok_rows, cut), bf16),
-            few, few, few, few,
+            few, few, few, few, few,
             pltpu.VMEM((width, 2, cols), bf16),
             pltpu.VMEM((width, 2 * cols), bf16),
             pltpu.VMEM((cols, width), bf16),
@@ -546,11 +544,11 @@
             pltpu.VMEM((parts, 8, count), f32),
             pltpu.VMEM((8, count), f32),
             dma((4,)), hop, hop, hop, hop, hop, dma((2, parts, slices)),
-            each, each, each, some, some, some, some,
+            each, each, each, some, some, some, some, some,
             dma((parts,)), dma((parts,)),
         ],
         compiler_params=pltpu.CompilerParams(
-            collective_id=0, has_side_effects=True, vmem_limit_bytes=53477376
+            collective_id=0, has_side_effects=True, vmem_limit_bytes=54 << 20
         ),
     )(tokens, norm_gain[None, :], final_gain[None, :], value_head[None, :], owner[None, :], lengths[None, :],
       offsets[None, :], w_in[0], w_down[0])

time: 90.1 us -> 85.2 us (0.946)
  local copies, waits for them, and re-layouts: 5.57 us -> 2.83 us
  Pallas kernels: 82.8 us -> 80.9 us
    unnamed x14 -> x2, local copies, waits for them, and re-layouts: 5.57 us -> 2.83 us
    pallas_call x1, Pallas kernels: 82.8 us -> 80.9 us  [mega_rows(): pl.pallas_call(functools.partial(mega_kernel, levels, cuts, slices), out_...]
where the time goes in v4:
time: 85.2 us; the launch traced here: 85 us
  Pallas kernels  80.9 us (95%)
  local copies, waits for them, and re-layouts  2.83 us (3%)
  between operations  1.29 us (2%)
    pallas_call x1, Pallas kernels, mega_rows(): pl.pallas_call(functools.partial(mega_kernel, levels, cuts, slices), out_...  80.9 us
    unnamed x2, local copies, waits for them, and re-layouts  2.83 us

profile of v4, /device:TPU:0, one launch (start us, length us, event | category | flops | bytes accessed | tf_op | source)
XLA Modules:
  0.0 85.0 jit_solution(7545649943913382221)
XLA Ops:
  1.3 80.9 %shard_map.104 = (bf16[40,3072]{1,0:T(8,128)(2,1)}, f32[1,8]{1,0:T(1,128)}) custom-call(bf16[40,3072]{1,0:T(8,128)(2,1)} %tok_ref.1, f32[1,3072]{1,0:T(1,128)} %bitcast.12, f32[1,3072]{1,0:T(1,128)} %bitcast.13, f32[1,3072]{1,0:T(1,128)} %bitcast.14, s32[1,1]{1,0:T(1,128)} %bitcast.9.owner_ref, s32[1,8]{1,0:T(1,128)} %bitcast.15, s32[1,8]{1,0:T(1,128)} %bitcast.16, ...), custom_call_target="tpu_custom_call" | custom-call | tf_op jit(solution)/shard_map/pallas_call | solution.py:526
  82.2 1.7 %copy.14 = bf16[40,3072]{1,0:T(8,128)(2,1)} copy(bf16[40,3072]{1,0:T(8,128)(2,1)} %get-tuple-element.8) | data formatting | bytes 491520
  83.9 1.2 %copy.15 = f32[8]{0:T(128)} copy(f32[8]{0:T(128)} %bitcast.17) | data formatting | bytes 64

commit v5 on v4

--- a/solution.py
+++ b/solution.py
@@ -83,7 +83,7 @@
                 wdown_ref, mixed_ref, rewards_ref,
                 x_buf, part, swap_buf, cross_buf, first_buf, second_buf, level_buf, near_buf, raw, win, wdown, hid,
                 acc, mean_buf, own_mean,
-                w_sem, up_send, down_send, first_send, second_send, pass_send, recv_sem,
+                w_sem, up_send, down_send, first_send, second_send, pass_send, recv_sem, hand_recv,
                 swap_send, swap_recv, sum_send, cross_recv, first_recv, second_recv, level_recv, near_recv,
                 mean_send, mean_recv):
     rep, slot = lax.axis_index("rep"), lax.axis_index("mp")
@@ -163,25 +163,26 @@
         return x_buf.at[index, plane, :, pl.ds(s * slab, slab)]
 
     def move(index, s, sem, column, at):
-        return remote(piece(index, side, s), piece(index, side, s), sem.at[index, s], recv_sem.at[side, index, s],
-                      column, at, side)
+        return remote(piece(index, side, s), piece(index, side, s), sem, recv_sem.at[index, s], column, at, side)
 
     def hand(index, s):
-        return remote(piece(index, side, s), piece(index, side, s), pass_send.at[index, s],
-                      recv_sem.at[side, index, s], here, level, twin)
+        return remote(piece(index, side, s), piece(index, side, s), pass_send,
+                      hand_recv.at[index // 4], here, level, twin)
+
+    def wait_for(ref, sem):
+        pltpu.make_async_copy(ref, ref, sem).wait()
 
     def arrive(plane, index, s):
-        at = piece(index, plane, s)
-        pltpu.make_async_copy(at, at, recv_sem.at[plane, index, s]).wait()
+        wait_for(piece(index, plane, s), recv_sem.at[index, s])
 
     def pass_on(index, s, upward, downward):
         @pl.when(upward & (level < levels - 1))
         def _():
-            move(index, s, up_send, here, level + 1).start()
+            move(index, s, up_send.at[index // 4, index % 4, s], here, level + 1).start()
 
         @pl.when(downward & (level > 0))
         def _():
-            move(index, s, down_send, here, level - 1).start()
+            move(index, s, down_send.at[index // 4, index % 4, s], here, level - 1).start()
 
         move(index, s, second_send, second, level).start()
         hand(index, s).start()
@@ -198,9 +199,8 @@
         hand(index, s).start()
 
     def collect_hands(d):
-        for column in (here, first, second, cross):
-            for s in range(slices):
-                arrive(twin, index_of(column, from_level(d)), s)
+        at = from_level(d)
+        wait_for(x_buf.at[pl.ds(at * 4, 4), twin], hand_recv.at[at])
 
     up_block = 256
 
@@ -228,11 +228,11 @@
             swap(index_of(column, at), q).start()
 
     def swap(index, q):
-        return remote(part.at[q, index, twin], swap_buf.at[q, index], swap_send.at[q, index],
+        return remote(part.at[q, index, twin], swap_buf.at[q, index], swap_send,
                       swap_recv.at[q, index], here, level, twin)
 
     def send(index, q, buf, sem, at, column, to):
-        return remote(swap_buf.at[q, index], buf.at[q, at], sum_send.at[q, index], sem.at[q, at], column, to, side)
+        return remote(swap_buf.at[q, index], buf.at[q, at], sum_send, sem.at[q, at], column, to, side)
 
     def landed(buf, sem, q, at):
         pltpu.make_async_copy(buf.at[q, at], buf.at[q, at], sem.at[q, at]).wait()
@@ -453,8 +453,8 @@
     def tell(d):
         to = (slot + d) % parts
         return pltpu.make_async_remote_copy(
-            src_ref=own_mean, dst_ref=mean_buf.at[slot], send_sem=mean_send.at[to],
-            recv_sem=mean_recv.at[slot], device_id=(rep, to), device_id_type=MESH,
+            src_ref=own_mean, dst_ref=mean_buf.at[slot], send_sem=mean_send,
+            recv_sem=mean_recv, device_id=(rep, to), device_id_type=MESH,
         )
 
     @pl.loop(1, parts)
@@ -463,53 +463,34 @@
 
     mixed_ref[...] = resid.astype(jnp.bfloat16)
     acc[:8, :count] = own_mean[...]
-    @pl.loop(0, slices)
-    def _(s):
-        move(mine, s, first_send, first, level).wait_send()
-
-        @pl.loop(0, levels)
-        def _(d):
+    @pl.loop(0, levels)
+    def _(d):
+        for s in range(slices):
             for column in (here, first):
                 index = index_of(column, d)
-                move(index, s, second_send, second, level).wait_send()
 
                 @pl.when((d <= level) & (level < levels - 1))
                 def _():
-                    move(index, s, up_send, here, level).wait_send()
+                    move(index, s, up_send.at[index // 4, index % 4, s], here, level).wait_send()
 
                 @pl.when((d >= level) & (level > 0))
                 def _():
-                    move(index, s, down_send, here, level).wait_send()
-
-    @pl.loop(0, parts)
-    def _(i):
-        for s in range(slices):
-            hand(i, s).wait_send()
-        for q in range(cuts):
-            swap(i, q).wait_send()
-
-    @pl.loop(0, levels)
-    def _(d):
-        for q in range(cuts):
-            for column in (cross, second, first):
-                send(index_of(column, d), q, cross_buf, cross_recv, level, second, level).wait_send()
-
-    @pl.loop(1, levels)
-    def _(d):
-        for q in range(cuts):
-            send(index_of(here, (level + d) % levels), q, level_buf, level_recv, level, second, level).wait_send()
+                    move(index, s, down_send.at[index // 4, index % 4, s], here, level).wait_send()
+
+    wait_for(x_buf.at[mine, side], first_send)
+    wait_for(x_buf.at[pl.ds(0, levels)], second_send)
+    wait_for(x_buf.at[pl.ds(0, parts // 2)], pass_send)
+    wait_for(swap_buf, swap_send)
+    wait_for(swap_buf.at[:, pl.ds(0, parts - 1)], sum_send)
+    wait_for(mean_buf.at[pl.ds(0, parts - 1)], mean_recv)
 
     @pl.loop(1, parts)
     def _(d):
-        index = (slot + parts - d) % parts
-        pltpu.make_async_copy(own_mean, mean_buf.at[index], mean_recv.at[index]).wait()
-        acc[:8, :count] += mean_buf[index]
+        acc[:8, :count] += mean_buf[(slot + parts - d) % parts]
 
     rewards_ref[...] = acc[:1, :count] / lengths_ref[...].astype(jnp.float32)
 
-    @pl.loop(1, parts)
-    def _(d):
-        tell(d).wait_send()
+    wait_for(mean_buf.at[pl.ds(0, parts - 1)], mean_send)
 
 
 def mega_rows(reps, parts, tokens, w_in, w_down, norm_gain, final_gain, value_head, owner, lengths, offsets):
@@ -543,9 +524,9 @@
             pltpu.VMEM((tok_rows, width), f32),
             pltpu.VMEM((parts, 8, count), f32),
             pltpu.VMEM((8, count), f32),
-            dma((4,)), hop, hop, hop, hop, hop, dma((2, parts, slices)),
-            each, each, each, some, some, some, some, some,
-            dma((parts,)), dma((parts,)),
+            dma((4,)), dma((levels, 4, slices)), dma((levels, 4, slices)), dma, dma, dma, hop, dma((levels,)),
+            dma, each, dma, some, some, some, some, some,
+            dma, dma,
         ],
         compiler_params=pltpu.CompilerParams(
             collective_id=0, has_side_effects=True, vmem_limit_bytes=54 << 20

time: 85.2 us -> 83.6 us (0.981)
  Pallas kernels: 80.9 us -> 79.3 us
    pallas_call x1, Pallas kernels: 80.9 us -> 79.3 us  [mega_rows(): pl.pallas_call(functools.partial(mega_kernel, levels, cuts, slices), out_...]
where the time goes in v5:
time: 83.6 us; the launch traced here: 83.4 us
  Pallas kernels  79.3 us (95%)
  local copies, waits for them, and re-layouts  2.83 us (3%)
  between operations  1.29 us (2%)
    pallas_call x1, Pallas kernels, mega_rows(): pl.pallas_call(functools.partial(mega_kernel, levels, cuts, slices), out_...  79.3 us
    unnamed x2, local copies, waits for them, and re-layouts  2.83 us

profile of v5, /device:TPU:0, one launch (start us, length us, event | category | flops | bytes accessed | tf_op | source)
XLA Modules:
  0.0 83.4 jit_solution(3330276786466315759)
XLA Ops:
  1.3 79.3 %shard_map.104 = (bf16[40,3072]{1,0:T(8,128)(2,1)}, f32[1,8]{1,0:T(1,128)}) custom-call(bf16[40,3072]{1,0:T(8,128)(2,1)} %tok_ref.1, f32[1,3072]{1,0:T(1,128)} %bitcast.12, f32[1,3072]{1,0:T(1,128)} %bitcast.13, f32[1,3072]{1,0:T(1,128)} %bitcast.14, s32[1,1]{1,0:T(1,128)} %bitcast.9.owner_ref, s32[1,8]{1,0:T(1,128)} %bitcast.15, s32[1,8]{1,0:T(1,128)} %bitcast.16, ...), custom_call_target="tpu_custom_call" | custom-call | tf_op jit(solution)/shard_map/pallas_call | solution.py:507
  80.6 1.7 %copy.14 = bf16[40,3072]{1,0:T(8,128)(2,1)} copy(bf16[40,3072]{1,0:T(8,128)(2,1)} %get-tuple-element.8) | data formatting | bytes 491520
  82.3 1.2 %copy.15 = f32[8]{0:T(128)} copy(f32[8]{0:T(128)} %bitcast.17) | data formatting | bytes 64

commit v6 on v5

--- a/solution.py
+++ b/solution.py
@@ -229,7 +229,7 @@
 
     def swap(index, q):
         return remote(part.at[q, index, twin], swap_buf.at[q, index], swap_send,
-                      swap_recv.at[q, index], here, level, twin)
+                      swap_recv.at[q, index // 4], here, level, twin)
 
     def send(index, q, buf, sem, at, column, to):
         return remote(swap_buf.at[q, index], buf.at[q, at], sum_send, sem.at[q, at], column, to, side)
@@ -238,7 +238,6 @@
         pltpu.make_async_copy(buf.at[q, at], buf.at[q, at], sem.at[q, at]).wait()
 
     def both(index, q):
-        swap(index, q).wait_recv()
         return part[q, index, side].astype(jnp.float32) + swap_buf[q, index].astype(jnp.float32)
 
     def reduce_outer(d, q, column, buf, sem):
@@ -248,6 +247,8 @@
         send(index, q, buf, sem, at, second, level).start()
 
     def reduce_cross(d, q):
+        at = from_level(d)
+        wait_for(swap_buf.at[q, pl.ds(at * 4, 4)], swap_recv.at[q, at])
         reduce_outer(d, q, cross, cross_buf, cross_recv)
 
     def reduce_second(d, q):
@@ -525,7 +526,7 @@
             pltpu.VMEM((parts, 8, count), f32),
             pltpu.VMEM((8, count), f32),
             dma((4,)), dma((levels, 4, slices)), dma((levels, 4, slices)), dma, dma, dma, hop, dma((levels,)),
-            dma, each, dma, some, some, some, some, some,
+            dma, some, dma, some, some, some, some, some,
             dma, dma,
         ],
         compiler_params=pltpu.CompilerParams(

time: 83.6 us -> 84.2 us (level)
  no operation moved by 1% of the time
where the time goes in v6:
time: 84.2 us; the launch traced here: 84 us
  Pallas kernels  79.9 us (95%)
  local copies, waits for them, and re-layouts  2.83 us (3%)
  between operations  1.29 us (2%)
    pallas_call x1, Pallas kernels, mega_rows(): pl.pallas_call(functools.partial(mega_kernel, levels, cuts, slices), out_...  79.9 us
    unnamed x2, local copies, waits for them, and re-layouts  2.83 us

profile of v6, /device:TPU:0, one launch (start us, length us, event | category | flops | bytes accessed | tf_op | source)
XLA Modules:
  0.0 84.0 jit_solution(10242319935465634696)
XLA Ops:
  1.3 79.9 %shard_map.104 = (bf16[40,3072]{1,0:T(8,128)(2,1)}, f32[1,8]{1,0:T(1,128)}) custom-call(bf16[40,3072]{1,0:T(8,128)(2,1)} %tok_ref.1, f32[1,3072]{1,0:T(1,128)} %bitcast.12, f32[1,3072]{1,0:T(1,128)} %bitcast.13, f32[1,3072]{1,0:T(1,128)} %bitcast.14, s32[1,1]{1,0:T(1,128)} %bitcast.9.owner_ref, s32[1,8]{1,0:T(1,128)} %bitcast.15, s32[1,8]{1,0:T(1,128)} %bitcast.16, ...), custom_call_target="tpu_custom_call" | custom-call | tf_op jit(solution)/shard_map/pallas_call | solution.py:508
  81.1 1.7 %copy.14 = bf16[40,3072]{1,0:T(8,128)(2,1)} copy(bf16[40,3072]{1,0:T(8,128)(2,1)} %get-tuple-element.8) | data formatting | bytes 491520
  82.8 1.2 %copy.15 = f32[8]{0:T(128)} copy(f32[8]{0:T(128)} %bitcast.17) | data formatting | bytes 64
